TPU v7x, 256 devices: a 2x2x32 block of a 4x8x32 slice. The times are simulated.
256 devices in a mesh: groups: 4 (over x, y), img: 32 (over z), space: 2 (over core).
Axes of the slice: x: 2, y: 2, z: 32, core: 2. Of those that a mesh axis runs over, the one named last changes fastest.
The devices are a block of a 4x8x32 slice.
Arguments:
- path: float32 [512, 64, 4096], P(('groups', 'img'), 'space'), parts along dimension 0, may hold values from -3 to 3
- bracket: int32 [512], P(('groups', 'img')), parts along dimension 0, may hold values from 0 to 126, as said below
Outputs:
- new_path: float32 [512, 64, 4096], P(('groups', 'img'), 'space'), parts along dimension 0
There are 4 independent parts, one for each index of `groups`. A program takes and returns all parts, laid end to end along the dimension named above; each array names one. Nothing has to cross between parts.
Inputs may be any that keep to these rules, and one draw needn't show every extreme that they name: bracket[j] differs from j by at most 2; it is given, not derived from the arc lengths, so the target arc length of image j need not lie between arc_b and arc_(b+1).
All inputs are finite; a program needn't handle non-finite values.
Results may differ from a plain program's by a relative error of at most 0.0003.
Values sent between devices are 32-bit elements; how exact they have to be, the bound alone decides.
A program may use at most 64 MiB of HBM per device.

v0:
```python
import jax
import jax.numpy as jnp
from jax import lax
from jax.sharding import PartitionSpec as P

REACH = 2
ITERS = 2


TIME_STEP = 0.002
EPSILON = 1e-06


def with_halo(block, sides, width, periodic):
    for axis, dim in sides:
        count = lax.axis_size(axis)
        forward = [(i, i + 1) for i in range(count - 1)]
        if periodic:
            forward.append((count - 1, 0))
        backward = [(target, source) for source, target in forward]
        low = lax.ppermute(
            lax.slice_in_dim(block, block.shape[dim] - width, None, axis=dim), axis, forward
        )
        high = lax.ppermute(lax.slice_in_dim(block, 0, width, axis=dim), axis, backward)
        block = jnp.concatenate([low, block, high], axis=dim)
    return block


def in_order(parts, dim):
    parts = jnp.moveaxis(parts, 0, dim)
    dims = parts.shape
    return parts.reshape(*dims[:dim], dims[dim] * dims[dim + 1], *dims[dim + 2 :])


def copy_for_each(x, axis):
    count = lax.axis_size(axis)
    return lax.all_to_all(jnp.broadcast_to(x[None], (count, *x.shape)), axis, 0, 0, tiled=True)


def gather_directly(x, axis, dim):
    return in_order(copy_for_each(x, axis), dim)


def laplace(field):
    padded = with_halo(field, (("space", 1),), 1, True)
    return (
        padded[:, 2:]
        + padded[:, :-2]
        + jnp.roll(field, 1, -1)
        + jnp.roll(field, -1, -1)
        - 4.0 * field
    )


def tangent_of(window, global_ids, count):
    center = window[1:-1]
    is_first = (global_ids == 0)[:, None, None]
    is_last = (global_ids == count - 1)[:, None, None]
    earlier = jnp.where(is_first, center, window[:-2])
    following = jnp.where(is_last, center, window[2:])
    stretch = jnp.where(is_first | is_last, jnp.float32(count - 1), jnp.float32((count - 1) / 2.0))
    return (following - earlier) * stretch


def theta_of(window, global_ids, count):
    center = window[1:-1]
    tangent = tangent_of(window, global_ids, count)
    drift_v = laplace(center) + center - center**3
    norm_sums = lax.psum(
        (jnp.sum(drift_v * drift_v, axis=(1, 2)), jnp.sum(tangent * tangent, axis=(1, 2))), "space"
    )
    speed = jnp.sqrt(norm_sums[0] + EPSILON) / jnp.sqrt(norm_sums[1] + EPSILON)
    return (speed[:, None, None] * tangent - drift_v, speed)


def per_device(path, bracket):
    local_count = path.shape[0]
    count = local_count * lax.axis_size("img")
    start = lax.axis_index("img") * local_count
    own_ids = start + jnp.arange(local_count)
    images = path
    for iteration in range(ITERS):
        window = with_halo(images, (("img", 0),), 1, False)
        theta, speed = theta_of(window, own_ids, count)
        theta_window = with_halo(theta, (("img", 0),), 1, False)
        descent = (
            speed[:, None, None] * tangent_of(theta_window, own_ids, count)
            + laplace(theta)
            + (1.0 - 3.0 * images * images) * theta
        )
        inside = ((own_ids > 0) & (own_ids < count - 1))[:, None, None]
        images = images + TIME_STEP * jnp.where(inside, descent, 0.0)
    margin = REACH + 1
    window = with_halo(images, (("img", 0),), margin, False)
    window_ids = start - margin + jnp.arange(local_count + 2 * margin)
    diffs = window[1:] - window[:-1]
    squares = lax.psum(jnp.sum(diffs * diffs, axis=(1, 2)), "space")
    counted = (window_ids[1:] >= 1) & (window_ids[1:] <= count - 1)
    segments = jnp.where(counted, jnp.sqrt(squares + EPSILON), 0.0)
    seg_full = jnp.concatenate([jnp.zeros((1,), segments.dtype), segments])
    running = jnp.cumsum(seg_full)
    own_length = running[margin + local_count - 1] - running[margin - 1]
    shares = gather_directly(own_length[None], "img", 0)
    device_ids = jnp.arange(shares.shape[0])
    offset = jnp.sum(jnp.where(device_ids < lax.axis_index("img"), shares, 0.0))
    length = jnp.sum(shares)
    arc_window = offset + running - running[margin - 1]
    target = length * own_ids.astype(segments.dtype) / (count - 1)
    local_pick = bracket - (start - margin)
    weight = (target - jnp.take(arc_window, local_pick)) / jnp.take(seg_full, local_pick + 1)
    base = jnp.take(window, local_pick, axis=0)
    upper = jnp.take(window, local_pick + 1, axis=0)
    return base + weight[:, None, None] * (upper - base)


def solution(mesh):
    return jax.shard_map(
        per_device,
        mesh=mesh,
        in_specs=(P(("groups", "img"), "space", None), P(("groups", "img"))),
        out_specs=P(("groups", "img"), "space", None),
        check_vma=False,
    )
```

profile of v0, /device:TPU:37, one launch (start us, length us, event | category | flops | bytes accessed | tf_op | source)
XLA Modules:
  0.0 221.4 jit_solution(6846588781592705991)
XLA Ops:
  0.0 2.4 %fusion.78 = (f32[1,32,4096]{2,1,0:T(8,128)}, f32[1,32,4096]{2,1,0:T(8,128)}) fusion(f32[4,32,4096]{2,1,0:T(8,128)} %param.6), kind=kLoop, calls=%fused_computation.125 | loop fusion | bytes 2097152 | tf_op jit(solution)/shard_map/slice | solution.py:24
  3.7 5.3 %collective-permute-start.3 = (f32[1,32,4096]{2,1,0:T(8,128)}, f32[1,32,4096]{2,1,0:T(8,128)S(1)}, u32[]{:S(2)}, u32[]{:S(2)}) collective-permute-start(f32[1,32,4096]{2,1,0:T(8,128)} %get-tuple-element.56), channel_id=1, source_target_pairs={{0,2},{2,4},{4,6},{6,8},{8,10},{10,12},{12,14},{14,16},{16,18},{18... | collective-permute-start | bytes 1572872 | tf_op jit(solution)/shard_map/ppermute | solution.py:21
  9.1 19.9 %collective-permute-start = (f32[4,1,4096]{2,1,0:T(1,128)S(1)}, f32[4,1,4096]{2,1,0:T(1,128)S(1)}, u32[]{:S(2)}, u32[]{:S(2)}) collective-permute-start(f32[4,1,4096]{2,1,0:T(1,128)S(1)} %get-tuple-element.57), channel_id=1, source_target_pairs={{1,0},{0,1},{3,2},{2,3},{5,4},{4,5},{7,6},{6,7},{9,8},{8,9},{11,10... | collective-permute-start | bytes 196616 | tf_op jit(solution)/shard_map/ppermute | solution.py:24
  29.1 2.8 %fusion.81 = (f32[4,32,4095]{2,1,0:T(8,128)}, f32[4,32,4095]{2,1,0:T(8,128)}) fusion(f32[4,32,4096]{2,1,0:T(8,128)S(1)} %copy-done.1), kind=kLoop, calls=%fused_computation.128 | loop fusion | bytes 8386560 | tf_op jit(solution)/shard_map/jit(_roll_static)/slice | solution.py:49
  32.0 5.6 %multiply_reduce_fusion.2 = (f32[4]{0:T(128)S(1)}, f32[4,32,4096]{2,1,0:T(8,128)}, f32[4]{0:T(128)S(1)}, f32[4,32,4096]{2,1,0:T(8,128)}) fusion(f32[4]{0:T(128)S(1)} %or_select_fusion, f32[4,32,4096]{2,1,0:T(8,128)S(1)} %copy-done.1, f32[1,32,4096]{2,1,0:T(8,128)S(1)} %collective-permute-done.3, pred[4]{0:T(512)(128)(4,1)S(1)} %get-tuple-element.69, ...), kind=kLoop, calls=%fused_computation.87 | loop fusion | flops 12058616 | bytes 11665464 | tf_op jit(solution)/shard_map/reduce_sum | solution.py:70
  37.6 5.8 %all-reduce.1 = (f32[4]{0:T(128)S(1)}, f32[4]{0:T(128)S(1)}) all-reduce(f32[4]{0:T(128)S(1)} %get-tuple-element.23, f32[4]{0:T(128)S(1)} %get-tuple-element.53), channel_id=1, replica_groups=mesh['groups'=4,'img'=32,'space'=2] {'space'}, use_global_device_ids=true, to_apply=%region_3.4 | all-reduce | flops 8 | bytes 64 | tf_op jit(solution)/shard_map/psum | solution.py:69
  43.4 2.5 %multiply_subtract_fusion.1 = f32[4,32,4096]{2,1,0:T(8,128)S(1)} fusion(f32[4,32,4096]{2,1,0:T(8,128)} %get-tuple-element.54, f32[4,32,4096]{2,1,0:T(8,128)} %get-tuple-element.24, f32[4]{0:T(128)S(1)} %rsqrt_multiply_fusion.1), kind=kLoop, calls=%fused_computation.86 | loop fusion | flops 1048576 | bytes 6291472 | tf_op jit(solution)/shard_map/sub | solution.py:73
  46.8 1.4 collective-permute-start.4
  48.2 4.7 %collective-permute-start.5 = (f32[1,32,4096]{2,1,0:T(8,128)S(1)}, f32[1,32,4096]{2,1,0:T(8,128)S(1)}, u32[]{:S(2)}, u32[]{:S(2)}) collective-permute-start(f32[1,32,4096]{2,1,0:T(8,128)S(1)} %get-tuple-element.50), channel_id=1, source_target_pairs={{0,2},{2,4},{4,6},{6,8},{8,10},{10,12},{12,14},{14,16},{16,18},{18... | collective-permute-start | bytes 1572872 | tf_op jit(solution)/shard_map/ppermute | solution.py:21
  55.0 7.8 %collective-permute-done.4 = f32[1,32,4096]{2,1,0:T(8,128)S(1)} collective-permute-done((f32[1,32,4096]{2,1,0:T(8,128)S(1)}, f32[1,32,4096]{2,1,0:T(8,128)S(1)}, u32[]{:S(2)}, u32[]{:S(2)}) %collective-permute-start.4) | collective-permute-done | bytes 524320 | tf_op jit(solution)/shard_map/ppermute | solution.py:24
  63.8 2.5 %fusion.8 = f32[4,32,4096]{2,1,0:T(8,128)S(1)} fusion(f32[4,32,4096]{2,1,0:T(8,128)S(1)} %copy-done.2, f32[4,32,4096]{2,1,0:T(8,128)S(1)} %multiply_subtract_fusion.1, f32[4,1,4096]{2,1,0:T(1,128)S(1)} %collective-permute-done.7, f32[4,1,4096]{2,1,0:T(1,128)S(1)} %collective-permute-done.6, f32[1,32,4096]{2,1,0:T(8,128)S(1)} %collective-permute-done.5, ...), kind=kLoop, calls=%fused_computation.18 | loop fusion | flops 13107200 | bytes 11665452 | tf_op jit(solution)/shard_map/add | solution.py:92
  68.5 4.8 %collective-permute-start.11 = (f32[1,32,4096]{2,1,0:T(8,128)S(1)}, f32[1,32,4096]{2,1,0:T(8,128)S(1)}, u32[]{:S(2)}, u32[]{:S(2)}) collective-permute-start(f32[1,32,4096]{2,1,0:T(8,128)S(1)} %get-tuple-element.38), channel_id=1, source_target_pairs={{0,2},{2,4},{4,6},{6,8},{8,10},{10,12},{12,14},{14,16},{16,18},{18... | collective-permute-start | bytes 1572872 | tf_op jit(solution)/shard_map/ppermute | solution.py:21
  73.4 1.6 collective-permute-start.8
  76.2 6.1 %collective-permute-done.10 = f32[1,32,4096]{2,1,0:T(8,128)S(1)} collective-permute-done((f32[1,32,4096]{2,1,0:T(8,128)S(1)}, f32[1,32,4096]{2,1,0:T(8,128)S(1)}, u32[]{:S(2)}, u32[]{:S(2)}) %collective-permute-start.10) | collective-permute-done | bytes 524320 | tf_op jit(solution)/shard_map/ppermute | solution.py:24
  83.3 4.0 %multiply_reduce_fusion = (f32[4]{0:T(128)S(1)}, f32[4,32,4096]{2,1,0:T(8,128)}, f32[4]{0:T(128)S(1)}, f32[4,32,4096]{2,1,0:T(8,128)}) fusion(f32[4]{0:T(128)S(1)} %or_select_fusion, f32[4,32,4096]{2,1,0:T(8,128)S(1)} %fusion.8, f32[1,32,4096]{2,1,0:T(8,128)S(1)} %collective-permute-done.11, pred[4]{0:T(512)(128)(4,1)S(1)} %get-tuple-element.69, ...), kind=kLoop, calls=%fused_computation.84 | loop fusion | flops 12058616 | bytes 11665464 | tf_op jit(solution)/shard_map/reduce_sum | solution.py:70
  87.3 4.4 %all-reduce = (f32[4]{0:T(128)S(1)}, f32[4]{0:T(128)S(1)}) all-reduce(f32[4]{0:T(128)S(1)} %get-tuple-element.19, f32[4]{0:T(128)S(1)} %get-tuple-element.35), channel_id=1, replica_groups=mesh['groups'=4,'img'=32,'space'=2] {'space'}, use_global_device_ids=true, to_apply=%region_7.8 | all-reduce | flops 8 | bytes 64 | tf_op jit(solution)/shard_map/psum | solution.py:69
  91.7 2.5 %multiply_subtract_fusion = f32[4,32,4096]{2,1,0:T(8,128)S(1)} fusion(f32[4,32,4096]{2,1,0:T(8,128)} %get-tuple-element.36, f32[4,32,4096]{2,1,0:T(8,128)} %get-tuple-element.20, f32[4]{0:T(128)S(1)} %rsqrt_multiply_fusion), kind=kLoop, calls=%fused_computation.83 | loop fusion | flops 1048576 | bytes 6291472 | tf_op jit(solution)/shard_map/sub | solution.py:73
  96.4 4.8 %collective-permute-start.13 = (f32[1,32,4096]{2,1,0:T(8,128)S(1)}, f32[1,32,4096]{2,1,0:T(8,128)S(1)}, u32[]{:S(2)}, u32[]{:S(2)}) collective-permute-start(f32[1,32,4096]{2,1,0:T(8,128)S(1)} %get-tuple-element.32), channel_id=1, source_target_pairs={{0,2},{2,4},{4,6},{6,8},{8,10},{10,12},{12,14},{14,16},{16,18},{18... | collective-permute-start | bytes 1572872 | tf_op jit(solution)/shard_map/ppermute | solution.py:21
  103.3 7.8 %collective-permute-done.12 = f32[1,32,4096]{2,1,0:T(8,128)S(1)} collective-permute-done((f32[1,32,4096]{2,1,0:T(8,128)S(1)}, f32[1,32,4096]{2,1,0:T(8,128)S(1)}, u32[]{:S(2)}, u32[]{:S(2)}) %collective-permute-start.12) | collective-permute-done | bytes 524320 | tf_op jit(solution)/shard_map/ppermute | solution.py:24
  112.1 2.5 %fusion.15 = f32[4,32,4096]{2,1,0:T(8,128)S(1)} fusion(f32[4,32,4096]{2,1,0:T(8,128)S(1)} %fusion.8, f32[4,32,4096]{2,1,0:T(8,128)S(1)} %multiply_subtract_fusion, f32[4,1,4096]{2,1,0:T(1,128)S(1)} %collective-permute-done.15, f32[4,1,4096]{2,1,0:T(1,128)S(1)} %collective-permute-done.14, f32[1,32,4096]{2,1,0:T(8,128)S(1)} %collective-permute-done.13, ...), kind=kLoop, calls=%fused_computation.25 | loop fusion | flops 13107200 | bytes 11665452 | tf_op jit(solution)/shard_map/add | solution.py:92
  114.6 2.3 %fusion.65 = (f32[3,32,4096]{2,1,0:T(8,128)}, f32[3,32,4096]{2,1,0:T(8,128)}) fusion(f32[4,32,4096]{2,1,0:T(8,128)S(1)} %fusion.15), kind=kLoop, calls=%fused_computation.112 | loop fusion | bytes 6291456 | tf_op jit(solution)/shard_map/slice | solution.py:22
  117.0 4.2 %collective-permute-start.16 = (f32[3,32,4096]{2,1,0:T(8,128)}, f32[3,32,4096]{2,1,0:T(8,128)S(1)}, u32[]{:S(2)}, u32[]{:S(2)}) collective-permute-start(f32[3,32,4096]{2,1,0:T(8,128)} %get-tuple-element.25), channel_id=1, source_target_pairs={{0,2},{2,4},{4,6},{6,8},{8,10},{10,12},{12,14},{14,16},{16,18},{18... | collective-permute-start | bytes 4718600 | tf_op jit(solution)/shard_map/ppermute | solution.py:21
  122.6 31.4 %collective-permute-done.16 = f32[3,32,4096]{2,1,0:T(8,128)S(1)} collective-permute-done((f32[3,32,4096]{2,1,0:T(8,128)}, f32[3,32,4096]{2,1,0:T(8,128)S(1)}, u32[]{:S(2)}, u32[]{:S(2)}) %collective-permute-start.16) | collective-permute-done | bytes 1572896 | tf_op jit(solution)/shard_map/ppermute | solution.py:21
  154.0 3.9 %collective-permute-done.17 = f32[3,32,4096]{2,1,0:T(8,128)S(1)} collective-permute-done((f32[3,32,4096]{2,1,0:T(8,128)}, f32[3,32,4096]{2,1,0:T(8,128)S(1)}, u32[]{:S(2)}, u32[]{:S(2)}) %collective-permute-start.17) | collective-permute-done | bytes 1572896 | tf_op jit(solution)/shard_map/ppermute | solution.py:24
  157.8 2.1 pad_maximum_fusion
  160.6 1.7 copy-done
  162.2 4.5 %psum.39 = f32[9]{0:T(128)S(1)} all-reduce(f32[9]{0:T(128)S(1)} %fusion.1), channel_id=1, replica_groups=mesh['groups'=4,'img'=32,'space'=2] {'space'}, use_global_device_ids=true, to_apply=%region_9.11 | all-reduce | flops 9 | bytes 72 | tf_op jit(solution)/shard_map/psum | solution.py:97
  169.5 24.1 %all-to-all-start = ((f32[32,1,1]{2,1,0:T(1,128)}), f32[32,1,1]{2,1,0:T(1,128)S(1)}, u32[]{:S(2)}, u32[]{:S(2)}) async-start(f32[32,1,1]{2,1,0:T(1,128)} %broadcast_in_dim.108), calls=%async_computation | async-start | bytes 32768 | tf_op jit(solution)/shard_map/all_to_all | solution.py:37
  193.6 3.2 %gather_fusion.3 = f32[4,32,4096]{2,1,0:T(8,128)S(1)} fusion(f32[10,32,4096]{2,1,0:T(8,128)} %copy-done, s32[1024]{0:T(1024)S(1)} %get-tuple-element.71), kind=kCustom, calls=%fused_computation.2.clone | custom fusion | bytes 4194320 | tf_op jit(solution)/shard_map/jit(_take)/gather | solution.py:112
  197.5 4.5 %gather_fusion = f32[4,32,4096]{2,1,0:T(8,128)} fusion(f32[10,32,4096]{2,1,0:T(8,128)} %copy-done, s32[1024]{0:T(1024)S(1)} %get-tuple-element.72), kind=kCustom, calls=%fused_computation.clone | custom fusion | bytes 4194320 | tf_op jit(solution)/shard_map/jit(_take)/gather | solution.py:111
  201.9 12.3 %all-to-all-done = f32[32,1,1]{2,1,0:T(1,128)S(1)} async-done(((f32[32,1,1]{2,1,0:T(1,128)}), f32[32,1,1]{2,1,0:T(1,128)S(1)}, u32[]{:S(2)}, u32[]{:S(2)}) %all-to-all-start) | async-done | bytes 160 | tf_op jit(solution)/shard_map/all_to_all | solution.py:37
  218.0 3.4 %fusion.55 = f32[4,32,4096]{2,1,0:T(8,128)} fusion(f32[4,32,4096]{2,1,0:T(8,128)S(1)} %gather_fusion.3, f32[4,32,4096]{2,1,0:T(8,128)} %gather_fusion, f32[4]{0:T(128)S(1)} %select_divide_fusion, pred[4]{0:T(512)(128)(4,1)S(1)} %get-tuple-element.67, pred[4]{0:T(512)(128)(4,1)S(1)} %get-tuple-element.13), kind=kLoop, calls=%fused_computation.82 | loop fusion | flops 2621440 | bytes 6291480 | tf_op jit(solution)/shard_map/add | solution.py:113
  (66 shorter events, 23.0 us)
Async XLA Ops:
  0.0 9.0 %copy-start.1 = (f32[4,32,4096]{2,1,0:T(8,128)S(1)}, f32[4,32,4096]{2,1,0:T(8,128)}, u32[]{:S(2)}) copy-start(f32[4,32,4096]{2,1,0:T(8,128)} %param.6) | copy-start | bytes 6291460
  2.4 29.6 %collective-permute-start.2 = (f32[1,32,4096]{2,1,0:T(8,128)}, f32[1,32,4096]{2,1,0:T(8,128)S(1)}, u32[]{:S(2)}, u32[]{:S(2)}) collective-permute-start(f32[1,32,4096]{2,1,0:T(8,128)} %get-tuple-element.55), channel_id=1, source_target_pairs={{2,0},{4,2},{6,4},{8,6},{10,8},{12,10},{14,12},{16,14},{18,16},{20... | collective-permute-start | bytes 1572872 | tf_op jit(solution)/shard_map/ppermute | solution.py:24
  3.7 28.3 %collective-permute-start.3 = (f32[1,32,4096]{2,1,0:T(8,128)}, f32[1,32,4096]{2,1,0:T(8,128)S(1)}, u32[]{:S(2)}, u32[]{:S(2)}) collective-permute-start(f32[1,32,4096]{2,1,0:T(8,128)} %get-tuple-element.56), channel_id=1, source_target_pairs={{0,2},{2,4},{4,6},{6,8},{8,10},{10,12},{12,14},{14,16},{16,18},{18... | collective-permute-start | bytes 1572872 | tf_op jit(solution)/shard_map/ppermute | solution.py:21
  9.1 22.9 %collective-permute-start = (f32[4,1,4096]{2,1,0:T(1,128)S(1)}, f32[4,1,4096]{2,1,0:T(1,128)S(1)}, u32[]{:S(2)}, u32[]{:S(2)}) collective-permute-start(f32[4,1,4096]{2,1,0:T(1,128)S(1)} %get-tuple-element.57), channel_id=1, source_target_pairs={{1,0},{0,1},{3,2},{2,3},{5,4},{4,5},{7,6},{6,7},{9,8},{8,9},{11,10... | collective-permute-start | bytes 196616 | tf_op jit(solution)/shard_map/ppermute | solution.py:24
  29.0 3.0 %collective-permute-start.1 = (f32[4,1,4096]{2,1,0:T(1,128)S(1)}, f32[4,1,4096]{2,1,0:T(1,128)S(1)}, u32[]{:S(2)}, u32[]{:S(2)}) collective-permute-start(f32[4,1,4096]{2,1,0:T(1,128)S(1)} %get-tuple-element.58), channel_id=1, source_target_pairs={{0,1},{1,0},{2,3},{3,2},{4,5},{5,4},{6,7},{7,6},{8,9},{9,8},{10,11... | collective-permute-start | bytes 196616 | tf_op jit(solution)/shard_map/ppermute | solution.py:21
  46.7 17.1 %copy-start.2 = (f32[4,32,4096]{2,1,0:T(8,128)S(1)}, f32[4,32,4096]{2,1,0:T(8,128)}, u32[]{:S(2)}) copy-start(f32[4,32,4096]{2,1,0:T(8,128)} %param.6) | copy-start | bytes 6291460
  46.8 16.1 %collective-permute-start.4 = (f32[1,32,4096]{2,1,0:T(8,128)S(1)}, f32[1,32,4096]{2,1,0:T(8,128)S(1)}, u32[]{:S(2)}, u32[]{:S(2)}) collective-permute-start(f32[1,32,4096]{2,1,0:T(8,128)S(1)} %get-tuple-element.49), channel_id=1, source_target_pairs={{2,0},{4,2},{6,4},{8,6},{10,8},{12,10},{14,12},{16,14},{18,16},{20... | collective-permute-start | bytes 1572872 | tf_op jit(solution)/shard_map/ppermute | solution.py:24
  48.2 15.6 %collective-permute-start.5 = (f32[1,32,4096]{2,1,0:T(8,128)S(1)}, f32[1,32,4096]{2,1,0:T(8,128)S(1)}, u32[]{:S(2)}, u32[]{:S(2)}) collective-permute-start(f32[1,32,4096]{2,1,0:T(8,128)S(1)} %get-tuple-element.50), channel_id=1, source_target_pairs={{0,2},{2,4},{4,6},{6,8},{8,10},{10,12},{12,14},{14,16},{16,18},{18... | collective-permute-start | bytes 1572872 | tf_op jit(solution)/shard_map/ppermute | solution.py:21
  53.0 1.6 collective-permute-start.6
  53.8 1.3 collective-permute-start.7
  67.1 15.2 %collective-permute-start.10 = (f32[1,32,4096]{2,1,0:T(8,128)S(1)}, f32[1,32,4096]{2,1,0:T(8,128)S(1)}, u32[]{:S(2)}, u32[]{:S(2)}) collective-permute-start(f32[1,32,4096]{2,1,0:T(8,128)S(1)} %get-tuple-element.37), channel_id=1, source_target_pairs={{2,0},{4,2},{6,4},{8,6},{10,8},{12,10},{14,12},{16,14},{18,16},{20... | collective-permute-start | bytes 1572872 | tf_op jit(solution)/shard_map/ppermute | solution.py:24
  68.5 14.8 %collective-permute-start.11 = (f32[1,32,4096]{2,1,0:T(8,128)S(1)}, f32[1,32,4096]{2,1,0:T(8,128)S(1)}, u32[]{:S(2)}, u32[]{:S(2)}) collective-permute-start(f32[1,32,4096]{2,1,0:T(8,128)S(1)} %get-tuple-element.38), channel_id=1, source_target_pairs={{0,2},{2,4},{4,6},{6,8},{8,10},{10,12},{12,14},{14,16},{16,18},{18... | collective-permute-start | bytes 1572872 | tf_op jit(solution)/shard_map/ppermute | solution.py:21
  73.4 2.5 %collective-permute-start.8 = (f32[4,1,4096]{2,1,0:T(1,128)S(1)}, f32[4,1,4096]{2,1,0:T(1,128)S(1)}, u32[]{:S(2)}, u32[]{:S(2)}) collective-permute-start(f32[4,1,4096]{2,1,0:T(1,128)S(1)} %get-tuple-element.39), channel_id=1, source_target_pairs={{1,0},{0,1},{3,2},{2,3},{5,4},{4,5},{7,6},{6,7},{9,8},{8,9},{11,10... | collective-permute-start | bytes 196616 | tf_op jit(solution)/shard_map/ppermute | solution.py:24
  75.0 1.3 collective-permute-start.9
  95.1 16.1 %collective-permute-start.12 = (f32[1,32,4096]{2,1,0:T(8,128)S(1)}, f32[1,32,4096]{2,1,0:T(8,128)S(1)}, u32[]{:S(2)}, u32[]{:S(2)}) collective-permute-start(f32[1,32,4096]{2,1,0:T(8,128)S(1)} %get-tuple-element.31), channel_id=1, source_target_pairs={{2,0},{4,2},{6,4},{8,6},{10,8},{12,10},{14,12},{16,14},{18,16},{20... | collective-permute-start | bytes 1572872 | tf_op jit(solution)/shard_map/ppermute | solution.py:24
  96.4 15.7 %collective-permute-start.13 = (f32[1,32,4096]{2,1,0:T(8,128)S(1)}, f32[1,32,4096]{2,1,0:T(8,128)S(1)}, u32[]{:S(2)}, u32[]{:S(2)}) collective-permute-start(f32[1,32,4096]{2,1,0:T(8,128)S(1)} %get-tuple-element.32), channel_id=1, source_target_pairs={{0,2},{2,4},{4,6},{6,8},{8,10},{10,12},{12,14},{14,16},{16,18},{18... | collective-permute-start | bytes 1572872 | tf_op jit(solution)/shard_map/ppermute | solution.py:21
  101.3 1.6 collective-permute-start.14
  102.0 1.3 collective-permute-start.15
  114.6 2.4 %copy-start.3 = (f32[4,32,4096]{2,1,0:T(8,128)}, f32[4,32,4096]{2,1,0:T(8,128)S(1)}, u32[]{:S(2)}) copy-start(f32[4,32,4096]{2,1,0:T(8,128)S(1)} %fusion.15) | copy-start | bytes 6291460
  114.6 7.9 %copy-start.4 = (s32[4]{0:T(128)S(1)}, s32[4]{0:T(128)}, u32[]{:S(2)}) copy-start(s32[4]{0:T(128)} %param.7) | copy-start | bytes 52
  117.0 37.0 %collective-permute-start.16 = (f32[3,32,4096]{2,1,0:T(8,128)}, f32[3,32,4096]{2,1,0:T(8,128)S(1)}, u32[]{:S(2)}, u32[]{:S(2)}) collective-permute-start(f32[3,32,4096]{2,1,0:T(8,128)} %get-tuple-element.25), channel_id=1, source_target_pairs={{0,2},{2,4},{4,6},{6,8},{8,10},{10,12},{12,14},{14,16},{16,18},{18... | collective-permute-start | bytes 4718600 | tf_op jit(solution)/shard_map/ppermute | solution.py:21
  121.2 36.6 %collective-permute-start.17 = (f32[3,32,4096]{2,1,0:T(8,128)}, f32[3,32,4096]{2,1,0:T(8,128)S(1)}, u32[]{:S(2)}, u32[]{:S(2)}) collective-permute-start(f32[3,32,4096]{2,1,0:T(8,128)} %get-tuple-element.26), channel_id=1, source_target_pairs={{2,0},{4,2},{6,4},{8,6},{10,8},{12,10},{14,12},{16,14},{18,16},{20... | collective-permute-start | bytes 4718600 | tf_op jit(solution)/shard_map/ppermute | solution.py:24
  159.9 2.3 %copy-start = (f32[10,32,4096]{2,1,0:T(8,128)}, f32[10,32,4096]{2,1,0:T(8,128)S(1)}, u32[]{:S(2)}) copy-start(f32[10,32,4096]{2,1,0:T(8,128)S(1)} %pad_maximum_fusion) | copy-start | bytes 15728644
  169.5 44.7 %all-to-all-start = ((f32[32,1,1]{2,1,0:T(1,128)}), f32[32,1,1]{2,1,0:T(1,128)S(1)}, u32[]{:S(2)}, u32[]{:S(2)}) async-start(f32[32,1,1]{2,1,0:T(1,128)} %broadcast_in_dim.108), calls=%async_computation | async-start | bytes 32768 | tf_op jit(solution)/shard_map/all_to_all | solution.py:37
where the time goes:
time: 222 us; the launch traced here: 221 us
  starting transfers between devices  78.2 us (35%)
  waiting for transfers between devices  75.3 us (34%)
  other arithmetic  29.3 us (13%)
  local copies, waits for them, and re-layouts  22.4 us (10%)
  blocking collectives  14.6 us (7%)
    ppermute x9, waiting for transfers between devices, with_halo(): lax.ppermute(lax.slice_in_dim(block, block.shape[dim] - width, None, axis...  35.3 us
    ppermute x9, starting transfers between devices, with_halo(): lax.ppermute(lax.slice_in_dim(block, 0, width, axis=dim), axis, backward)  29.6 us
    ppermute x9, waiting for transfers between devices, with_halo(): lax.ppermute(lax.slice_in_dim(block, 0, width, axis=dim), axis, backward)  27.7 us
    ppermute x9, starting transfers between devices, with_halo(): lax.ppermute(lax.slice_in_dim(block, block.shape[dim] - width, None, axis...  24.4 us
    all_to_all x1, starting transfers between devices, copy_for_each(): lax.all_to_all(jnp.broadcast_to(x[None], (count, *x.shape)), axis, 0, 0,...  24.1 us
    all_to_all x1, waiting for transfers between devices, copy_for_each(): lax.all_to_all(jnp.broadcast_to(x[None], (count, *x.shape)), axis, 0, 0,...  12.3 us
    psum x2, blocking collectives, theta_of(): lax.psum((jnp.sum(drift_v * drift_v, axis=(1, 2)), jnp.sum(tangent * tang...  10.2 us
    reduce_sum x2, other arithmetic, theta_of(): jnp.sum(tangent * tangent, axis=(1, 2))  9.63 us
  transfers between devices with their start and end apart: 19, of which 15 were waited for; matrix products, arithmetic and copies ran while one was open for 5% of the time, Pallas kernels for 0%

commit v1 on v0

v1 whole, which is shorter than its diff:
```python
import functools

import jax
import jax.numpy as jnp
from jax import lax
from jax.experimental import pallas as pl
from jax.experimental.pallas import tpu as pltpu
from jax.sharding import PartitionSpec as P

REACH = 2
ITERS = 2
TIME_STEP = 0.002
EPSILON = 1e-06

LANES = 128
SUB = 8
OWN = 4
TILES = 4
EXT = TILES + 1
FIRST = 4
WINDOW = OWN + 2 * FIRST


def fold(block):
    parts = [block[:, i : i + LANES] for i in range(0, block.shape[1], LANES)]
    while len(parts) > 1:
        parts = [a + b for a, b in zip(parts[::2], parts[1::2])] + parts[len(parts) // 2 * 2 :]
    return parts[0]


def spread(vector, width):
    return jnp.concatenate([vector] * (width // LANES), axis=1)


def kernel(count, axes, path, bracket, out, phi0, phi1, phi2_0, phi2_1, phi2_2, phi2_3, th0, th1, rows_in, mine0, theirs0, mine1, theirs1,
           mine2, theirs2, speed0, speed1, message, gathered, result,
           local_sem, up_send, up_recv, down_send, down_recv, row_send, row_recv, sum_send, sum_recv,
           new_send, new_recv, len_send, len_recv, out_sem, live):
    cols = path.shape[-1]
    half = min(cols, 1024)
    phi2 = (phi2_0, phi2_1, phi2_2, phi2_3)
    img = lax.axis_index("img")
    core = lax.axis_index("space")

    low = lax.rem(img + count - 1, count)
    high = lax.rem(img + 1, count)
    partner = 1 - core
    to_low, to_high, to_partner = {"img": low}, {"img": high}, {"space": partner}
    mesh_id = pl.DeviceIdType.MESH

    def remote(src, dst, send, recv, where):
        return pltpu.make_async_remote_copy(
            src_ref=src, dst_ref=dst, send_sem=send, recv_sem=recv, device_id=where, device_id_type=mesh_id
        )

    loads = [
        pltpu.make_async_copy(path.at[i], phi0.at[FIRST + i, pl.ds(0, TILES)], local_sem.at[i]) for i in range(OWN)
    ]
    for i in (0, 3, 1, 2):
        loads[i].start()

    barrier = pltpu.get_barrier_semaphore()
    for where in (to_low, to_high, to_partner):
        pl.semaphore_signal(barrier, inc=1, device_id=where, device_id_type=mesh_id)
    pl.semaphore_wait(barrier, 3)

    own = lambda image: phi0.at[image, pl.ds(0, TILES)]
    down = [
        remote(own(FIRST + i), own(FIRST + OWN + i), down_send.at[i], down_recv.at[i], to_low) for i in range(OWN)
    ]
    up = [remote(own(FIRST + i), own(i), up_send.at[i], up_recv.at[i], to_high) for i in range(OWN)]

    def row_copies(image):
        return [
            remote(phi0.at[image, tile], rows_in.at[image, k], row_send.at[image, k], row_recv.at[image, k], to_partner)
            for k, tile in enumerate((0, TILES - 1))
        ]

    row_moves = {image: row_copies(image) for image in range(1, WINDOW - 1)}

    for i in (0, 3, 1, 2):
        loads[i].wait()
        if i == 0:
            down[0].start()
        elif i == 3:
            up[3].start()
    for i in range(1, OWN):
        down[i].start()
        up[OWN - 1 - i].start()
    for image in range(FIRST, FIRST + OWN):
        for copy in row_moves[image]:
            copy.start()
    far = 1
    step = 0
    lives = []
    while 2 * far < count + 1 and far < count // 2:
        lives.append(far)
        far *= 2

    def say_live(step):
        distance = lives[step]
        for other in (lax.rem(img + distance, count), lax.rem(img + count - distance, count)):
            pl.semaphore_signal(live.at[step], inc=1, device_id={"img": other}, device_id_type=mesh_id)

    def hear_live(step):
        pl.semaphore_wait(live.at[step], 2)

    if lives:
        say_live(0)

    sub = lax.broadcasted_iota(jnp.int32, (SUB, half), 0)
    chunks = range(0, cols, half)

    is_first = (img == 0).astype(jnp.int32)
    is_last = (img == count - 1).astype(jnp.int32)
    last = OWN * count - 1

    def sides(image):
        at_first = is_first * (image == FIRST).astype(jnp.int32)
        at_last = is_last * (image == FIRST + OWN - 1).astype(jnp.int32)
        end = (at_first + at_last).astype(jnp.float32)
        return image - 1 + at_first, image + 1 - at_last, (1.0 + end) * jnp.float32(last / 2.0)

    def around(ref, slot, tile, c):
        above = lax.rem(tile + EXT - 1, EXT)
        below = lax.rem(tile + 1, EXT)
        here = ref[slot, tile, :, c : c + half]
        up_rows = pltpu.roll(jnp.where(sub == SUB - 1, ref[slot, above, :, c : c + half], here), 1, 0)
        down_rows = pltpu.roll(jnp.where(sub == 0, ref[slot, below, :, c : c + half], here), SUB - 1, 0)
        if half == cols:
            left = pltpu.roll(here, 1, 1)
            right = pltpu.roll(here, half - 1, 1)
        else:
            before = (c - LANES) % cols
            after = (c + half) % cols
            wide = jnp.concatenate(
                [ref[slot, tile, :, before : before + LANES], here, ref[slot, tile, :, after : after + LANES]], axis=1
            )
            left = pltpu.roll(wide, 1, 1)[:, LANES : LANES + half]
            right = pltpu.roll(wide, half + 2 * LANES - 1, 1)[:, LANES : LANES + half]
        return here, (up_rows + down_rows) + (left + right) - 4.0 * here

    zero = jnp.zeros((SUB, LANES), jnp.float32)

    def make_halo(image):
        for c in chunks:
            phi0[image, TILES, :, c : c + half] = jnp.where(
                sub < SUB // 2, rows_in[image, 0, :, c : c + half], rows_in[image, 1, :, c : c + half]
            )

    def drift(phi, th, slot, th_slot, tiles, total):
        def one(tile, acc):
            for c in chunks:
                here, lap = around(phi, slot, tile, c)
                force = lap + here - here * here * here
                th[th_slot, tile, :, c : c + half] = force
                acc = acc + jnp.where(tile < TILES, fold(force * force), 0.0)
            return acc

        total[...] = lax.fori_loop(0, tiles, one, zero)

    def stretch_sum(phi, lower, upper, total, factor):
        def one(tile, acc):
            for c in chunks:
                gap = phi[upper, tile, :, c : c + half] - phi[lower, tile, :, c : c + half]
                acc = acc + fold(gap * gap)
            return acc

        total[...] = lax.fori_loop(0, TILES, one, zero) * (factor * factor)

    def segment_sum(upper, total):
        acc = zero
        for ref in phi2:
            for c in chunks:
                gap = ref[upper, :, c : c + half] - ref[upper - 1, :, c : c + half]
                acc = acc + fold(gap * gap)
        total[...] = acc

    def theta(phi, th, lower, upper, factor, th_slot, speed, tiles):
        scale = spread(speed * factor, half)

        def one(tile, carry):
            for c in chunks:
                span = slice(c, c + half)
                gap = phi[upper, tile, :, span] - phi[lower, tile, :, span]
                th[th_slot, tile, :, span] = scale * gap - th[th_slot, tile, :, span]
            return carry

        lax.fori_loop(0, tiles, one, 0)

    def advance(phi, slot, th, th_slot, new, new_slot, speed, image, tiles):
        fixed = is_first * (image == FIRST).astype(jnp.int32) + is_last * (image == FIRST + OWN - 1).astype(jnp.int32)
        scale = spread(speed * jnp.float32(last / 2.0), half)

        def one(tile, carry):
            for c in chunks:
                span = slice(c, c + half)
                here, lap = around(th, th_slot, tile, c)
                old = phi[slot, tile, :, span]
                bend = th[th_slot + 1, tile, :, span] - th[th_slot - 1, tile, :, span]
                descent = scale * bend + lap + (1.0 - 3.0 * old * old) * here
                value = jnp.where(fixed == 0, old + TIME_STEP * descent, old)
                if new is phi2:
                    new[tile][new_slot, :, span] = value
                else:
                    new[new_slot, tile, :, span] = value
            return carry

        if new is phi2:
            for tile in range(tiles):
                one(tile, 0)
        else:
            lax.fori_loop(0, tiles, one, 0)

    def whole(a):
        return jnp.broadcast_to(jnp.sum(jnp.sum(a, axis=1, keepdims=True), axis=0, keepdims=True), (SUB, LANES))

    def speeds(mine, theirs, first, number, out_ref):
        for i in range(first, first + number):
            force = whole(mine[i, 0] + theirs[i, 0])
            stretch = whole(mine[i, 1] + theirs[i, 1])
            out_ref[i] = jnp.sqrt(force + EPSILON) / jnp.sqrt(stretch + EPSILON)

    def swap(mine, theirs, first, number, k):
        span = pl.ds(first, number)
        return remote(mine.at[span], theirs.at[span], sum_send.at[k], sum_recv.at[k], to_partner)

    p1, t0, t1 = lambda w: w - 2, lambda w: w - 1, lambda w: w - 3

    def place_of(image):
        outer_low = OWN + 2 * (FIRST - 1 - image)
        outer_high = OWN + 2 * (image - FIRST - OWN) + 1
        return jnp.where(image < FIRST, outer_low, jnp.where(image < FIRST + OWN, image - FIRST, outer_high))

    def each(images, body):
        start, step, number = images

        def one(i, carry):
            image = start + step * i
            body(image, place_of(image))
            return carry

        lax.fori_loop(0, number, one, 0)

    every = (FIRST, 1, OWN)
    inner = (FIRST + 1, 1, OWN - 2)

    def pair(n):
        return (FIRST - n, 2 * n + OWN - 1, 2)

    def pair_in(n):
        return pair(n - 1) if n > 1 else (FIRST, OWN - 1, 2)

    def gap0(image, place):
        lower, upper, factor = sides(image)
        stretch_sum(phi0, lower, upper, mine0.at[place, 1], factor)

    def drift0(tiles):
        def body(image, place):
            drift(phi0, th0, image, t0(image), tiles, mine0.at[place, 0])

        return body

    def theta0(tiles):
        def body(image, place):
            lower, upper, factor = sides(image)
            theta(phi0, th0, lower, upper, factor, t0(image), speed0[place], tiles)

        return body

    def next1(tiles):
        def body(image, _):
            advance(phi0, image, th0, t0(image), phi1, p1(image), speed0[place_of(image)], image, tiles)

        return body

    def gap1(image, _):
        lower, upper, factor = sides(image)
        stretch_sum(phi1, p1(lower), p1(upper), mine1.at[place_of(image), 1], factor)

    def drift1(tiles):
        def body(image, _):
            drift(phi1, th1, p1(image), t1(image), tiles, mine1.at[place_of(image), 0])

        return body

    def theta1(tiles):
        def body(image, _):
            lower, upper, factor = sides(image)
            theta(phi1, th1, p1(lower), p1(upper), factor, t1(image), speed1[place_of(image)], tiles)

        return body

    def next2(image, _):
        advance(phi1, p1(image), th1, t1(image), phi2, image - 2, speed1[place_of(image)], image, TILES)

    def arrive(n):
        down[n - 1].wait_recv()
        up[OWN - n].wait_recv()

    def halo(images):
        for image in images:
            for copy in row_moves[image]:
                copy.wait_recv()
            make_halo(image)

    halo(range(FIRST, FIRST + OWN))
    each(every, drift0(EXT))
    each(inner, gap0)

    swaps = []

    def exchange(mine, theirs, first, number):
        move = swap(mine, theirs, first, number, len(swaps))
        move.start()
        swaps.append(move)
        return move

    for n in range(1, FIRST + 1):
        outer = (FIRST - n, FIRST + OWN - 1 + n)
        arrive(n)
        if n < FIRST:
            for image in outer:
                for copy in row_moves[image]:
                    copy.start()
        each(pair_in(n), gap0)
        first, number = (0, OWN) if n == 1 else (OWN + 2 * (n - 2), 2)
        move = exchange(mine0, theirs0, first, number)
        if n < FIRST:
            halo(outer)
        move.wait_recv()
        speeds(mine0, theirs0, first, number, speed0)
        if n == 1:
            each(every, theta0(EXT))
            each(inner, next1(EXT))
        else:
            each(pair_in(n), theta0(EXT if n < FIRST else TILES))
            each(pair_in(n - 1), next1(EXT if n < FIRST else TILES))
        if n == 2:
            each(every, drift1(EXT))
            each(inner, gap1)
        if n >= 3:
            each(pair_in(n - 2), gap1)
            first, number = (0, OWN) if n == 3 else (OWN, 2)
            move = exchange(mine1, theirs1, first, number)
            move.wait_recv()
            speeds(mine1, theirs1, first, number, speed1)
            if n == 3:
                each(every, theta1(EXT))
                each(inner, next2)
            else:
                each(pair_in(2), theta1(TILES))
                each(pair_in(1), next2)
        if n == 3:
            down_new = []
            for k, (source, target) in enumerate(((5, 9), (6, 10), (4, 8))):
                down_new.append([
                    remote(phi2[t].at[source - 2], phi2[t].at[target - 2], new_send.at[k, t], new_recv.at[k, t], to_low)
                    for t in range(TILES)
                ])
            up_new = []
            for k, (source, target) in enumerate(((7, 3), (6, 2))):
                up_new.append([
                    remote(phi2[t].at[source - 2], phi2[t].at[target - 2], new_send.at[3 + k, t],
                           new_recv.at[3 + k, t], to_high)
                    for t in range(TILES)
                ])
            for k in (0, 1):
                for copy in down_new[k]:
                    copy.start()
        if n < FIRST:
            each(pair(n), drift0(EXT if n < FIRST - 1 else TILES))
        if n == 3:
            each(pair(1), drift1(TILES))
        if n <= len(lives):
            hear_live(n - 1)
            if n < len(lives):
                say_live(n)

    for k in (0, 1):
        for copy in up_new[k]:
            copy.start()
    for image in range(FIRST + 1, FIRST + OWN):
        segment_sum(image - 2, mine2.at[image - FIRST])
    for copy in up_new[0]:
        copy.wait_recv()
    segment_sum(2, mine2.at[0])
    move = exchange(mine2, theirs2, 0, OWN)
    move.wait_recv()

    lane = lax.broadcasted_iota(jnp.int32, (1, LANES), 1)
    lengths = jnp.zeros((1, LANES), jnp.float32)
    for i in range(OWN):
        segment = jnp.sqrt(whole(mine2[i] + theirs2[i])[0:1] + EPSILON)
        if i == 0:
            segment = jnp.where(img == 0, 0.0, segment)
        lengths = jnp.where(lane == i, segment, lengths)
    message[0] = lengths
    gathered[img] = lengths

    def send_length(k):
        return remote(message.at[0], gathered.at[img], len_send.at[k], len_recv.at[k], {"img": lax.rem(img + k, count)})

    def spread_out(i, carry):
        distance = count // 2 - 1 - i
        send_length(distance).start()
        send_length(count - distance).start()
        return carry

    send_length(count // 2).start()
    lax.fori_loop(0, count // 2 - 1, spread_out, 0)
    for copy in down_new[2]:
        copy.start()

    def heard(k, carry):
        send_length(k).wait_recv()
        return carry

    lax.fori_loop(1, count, heard, 0)

    owner = lax.broadcasted_iota(jnp.int32, (count, 1, LANES), 0)
    place = lax.broadcasted_iota(jnp.int32, (count, 1, LANES), 2)
    index = OWN * owner + place
    segs = jnp.where(place < OWN, gathered[...], 0.0)

    def add_up(a):
        return jnp.sum(jnp.sum(a, axis=0), axis=1, keepdims=True)

    length = add_up(segs)
    weights = []
    for i in range(OWN):
        base = bracket[i]
        arc = add_up(jnp.where(index <= base, segs, 0.0))
        seg = add_up(jnp.where(index == base + 1, segs, 0.0))
        target = length * (OWN * img + i).astype(jnp.float32) / jnp.float32(last)
        weights.append(jnp.broadcast_to((target - arc) / seg, (SUB, half)))

    writes = [pltpu.make_async_copy(result.at[t], out.at[t], out_sem.at[t]) for t in range(TILES)]
    for t in range(TILES):
        for k in (0, 1, 2):
            down_new[k][t].wait_recv()
        if t == 0:
            for copy in up_new[1]:
                copy.wait_recv()
        for i in range(OWN):
            pick = jnp.clip(bracket[i] - (OWN * img - 2), 0, WINDOW - 5)
            for c in chunks:
                span = slice(c, c + half)
                base = phi2[t][pick, :, span]
                result[t, i, :, span] = base + weights[i] * (phi2[t][pick + 1, :, span] - base)
        writes[t].start()

    for copy in down + up:
        copy.wait_send()
    for image in row_moves:
        for copy in row_moves[image]:
            copy.wait_send()
    for move in swaps:
        move.wait_send()
    for group in down_new + up_new:
        for copy in group:
            copy.wait_send()

    def sent(k, carry):
        send_length(k).wait_send()
        return carry

    lax.fori_loop(1, count, sent, 0)
    for copy in writes:
        copy.wait()


def per_device(count, axes, path, bracket):
    images, rows, cols = path.shape
    f32 = jnp.float32
    dma = pltpu.SemaphoreType.DMA
    tiled = path.reshape(images, TILES, SUB, cols)
    out = pl.pallas_call(
        functools.partial(kernel, count, axes),
        out_shape=jax.ShapeDtypeStruct((TILES, images, SUB, cols), f32),
        in_specs=[pl.BlockSpec(memory_space=pl.ANY), pl.BlockSpec(memory_space=pltpu.SMEM)],
        out_specs=pl.BlockSpec(memory_space=pl.ANY),
        scratch_shapes=[
            pltpu.VMEM((WINDOW, EXT, SUB, cols), f32),
            pltpu.VMEM((WINDOW - 4, EXT, SUB, cols), f32),
            *[pltpu.VMEM((WINDOW - 3, SUB, cols), f32) for _ in range(TILES)],
            pltpu.VMEM((WINDOW - 2, EXT, SUB, cols), f32),
            pltpu.VMEM((WINDOW - 6, EXT, SUB, cols), f32),
            pltpu.VMEM((WINDOW, 2, SUB, cols), f32),
            pltpu.VMEM((WINDOW, 2, SUB, LANES), f32),
            pltpu.VMEM((WINDOW, 2, SUB, LANES), f32),
            pltpu.VMEM((OWN + 2, 2, SUB, LANES), f32),
            pltpu.VMEM((OWN + 2, 2, SUB, LANES), f32),
            pltpu.VMEM((OWN, SUB, LANES), f32),
            pltpu.VMEM((OWN, SUB, LANES), f32),
            pltpu.VMEM((WINDOW, SUB, LANES), f32),
            pltpu.VMEM((WINDOW, SUB, LANES), f32),
            pltpu.VMEM((1, 1, LANES), f32),
            pltpu.VMEM((count, 1, LANES), f32),
            pltpu.VMEM((TILES, images, SUB, cols), f32),
            dma((OWN,)),
            dma((OWN,)),
            dma((OWN,)),
            dma((OWN,)),
            dma((OWN,)),
            dma((WINDOW, 2)),
            dma((WINDOW, 2)),
            dma((8,)),
            dma((8,)),
            dma((5, TILES)),
            dma((5, TILES)),
            dma((count,)),
            dma((count,)),
            dma((TILES,)),
            pltpu.SemaphoreType.REGULAR((8,)),
        ],
        compiler_params=pltpu.CompilerParams(
            collective_id=0, has_side_effects=True, vmem_limit_bytes=62 * 1024 * 1024
        ),
    )(tiled, bracket)
    return out.transpose(1, 0, 2, 3).reshape(images, rows, cols)


def solution(mesh):
    count = mesh.shape["img"]
    return jax.shard_map(
        functools.partial(per_device, count, tuple(mesh.axis_names)),
        mesh=mesh,
        in_specs=(P(("groups", "img"), "space", None), P(("groups", "img"))),
        out_specs=P(("groups", "img"), "space", None),
        check_vma=False,
    )
```

time: 222 us -> 115 us (0.52)
  Pallas kernels: 0 us -> 111 us
  starting transfers between devices: 78.2 us -> 0 us
  waiting for transfers between devices: 75.3 us -> 0 us
  other arithmetic: 29.3 us -> 0 us
  local copies, waits for them, and re-layouts: 22.4 us -> 3.11 us
  blocking collectives: 14.6 us -> 0 us
    pallas_call x0 -> x1, Pallas kernels: none -> 111 us  [per_device(): pl.pallas_call(functools.partial(kernel, count, axes), out_shape=jax.Shap...]
    ppermute x18 -> x0, waiting for transfers between devices: 63 us -> none  [the longest x9 35.3 us: with_halo(): lax.ppermute(lax.slice_in_dim(block, block.shape[dim] - width, None, axis...]
    ppermute x18 -> x0, starting transfers between devices: 54.1 us -> none  [the longest x9 29.6 us: with_halo(): lax.ppermute(lax.slice_in_dim(block, 0, width, axis=dim), axis, backward)]
    all_to_all x1 -> x0, starting transfers between devices: 24.1 us -> none  [copy_for_each(): lax.all_to_all(jnp.broadcast_to(x[None], (count, *x.shape)), axis, 0, 0,...]
    psum x3 -> x0, blocking collectives: 14.6 us -> none  [the longest x2 10.2 us: theta_of(): lax.psum((jnp.sum(drift_v * drift_v, axis=(1, 2)), jnp.sum(tangent * tang...]
    all_to_all x1 -> x0, waiting for transfers between devices: 12.3 us -> none  [copy_for_each(): lax.all_to_all(jnp.broadcast_to(x[None], (count, *x.shape)), axis, 0, 0,...]
    reduce_sum x5 -> x0, other arithmetic: 11.6 us -> none  [the longest x2 9.63 us: theta_of(): jnp.sum(tangent * tangent, axis=(1, 2))]
    slice x18 -> x0, local copies, waits for them, and re-layouts: 11.1 us -> none  [the longest x4 3.65 us: laplace(): jnp.roll(field, 1, -1)]
  transfers between devices with their start and end apart: 19 -> 0, of which waited for: 15 -> 0; matrix products, arithmetic and copies ran while one was open for 5% -> 0% of each run, Pallas kernels for 0% -> 0%
where the time goes in v1:
time: 115 us; the launch traced here: 114 us
  Pallas kernels  111 us (97%)
  local copies, waits for them, and re-layouts  3.11 us (3%)
    pallas_call x1, Pallas kernels, per_device(): pl.pallas_call(functools.partial(kernel, count, axes), out_shape=jax.Shap...  111 us
    reshape x1, local copies, waits for them, and re-layouts, per_device(): return out.transpose(1, 0, 2, 3).reshape(images, rows, cols)  3.11 us

profile of v1, /device:TPU:37, one launch (start us, length us, event | category | flops | bytes accessed | tf_op | source)
XLA Modules:
  0.0 114.0 jit_solution(294740072032188753)
XLA Ops:
  0.0 110.9 %shard_map.28 = f32[4,4,8,4096]{3,2,1,0:T(8,128)} custom-call(f32[4,4,8,4096]{3,2,1,0:T(8,128)} %bitcast.6, s32[4]{0:T(128)} %bracket.1), custom_call_target="tpu_custom_call" | custom-call | tf_op jit(solution)/shard_map/pallas_call | solution.py:478
  110.9 3.1 %copy_bitcast_fusion = f32[4,32,4096]{2,1,0:T(8,128)} fusion(f32[4,4,8,4096]{3,2,1,0:T(8,128)} %shard_map.28), kind=kLoop, calls=%fused_computation | loop fusion | bytes 4194304 | tf_op jit(solution)/shard_map/reshape | solution.py:521

commit v2 on v1

v2 whole, which is shorter than its diff:
```python
import functools

import jax
import jax.numpy as jnp
from jax import lax
from jax.experimental import pallas as pl
from jax.experimental.pallas import tpu as pltpu
from jax.sharding import PartitionSpec as P

REACH = 2
ITERS = 2
TIME_STEP = 0.002
EPSILON = 1e-06

LANES = 128
SUB = 8
OWN = 4
TILES = 4
EXT = TILES + 1
FIRST = 4


def fold(block):
    parts = [block[:, i : i + LANES] for i in range(0, block.shape[1], LANES)]
    while len(parts) > 1:
        parts = [a + b for a, b in zip(parts[::2], parts[1::2])] + parts[len(parts) // 2 * 2 :]
    return parts[0]


def spread(vector, width):
    return jnp.concatenate([vector] * (width // LANES), axis=1)


def kernel(count, path, bracket, out, phi0, phi1, phi2_0, phi2_1, phi2_2, phi2_3, th0, th1, rows0, rows1,
           mine0, theirs0, mine1, theirs1, mine2, theirs2, speed0, speed1, message, gathered, result,
           local_sem, down_send, down_recv, up_send, up_recv, row_send, row_recv, sum_send, sum_recv,
           new_send, new_recv, pace_send, pace_recv, len_send, len_recv, out_sem, live):
    cols = path.shape[-1]
    half = min(cols, 1024)
    phi2 = (phi2_0, phi2_1, phi2_2, phi2_3)
    img = lax.axis_index("img")
    core = lax.axis_index("space")

    low = lax.rem(img + count - 1, count)
    high = lax.rem(img + 1, count)
    partner = 1 - core
    to_low, to_high, to_partner = {"img": low}, {"img": high}, {"space": partner}
    mesh_id = pl.DeviceIdType.MESH

    def remote(src, dst, send, recv, where):
        return pltpu.make_async_remote_copy(
            src_ref=src, dst_ref=dst, send_sem=send, recv_sem=recv, device_id=where, device_id_type=mesh_id
        )

    p0, p1, p2, t0, t1 = (lambda w, s=s: w - s for s in (2, 1, 2, 3, 2))

    loads = [
        pltpu.make_async_copy(path.at[i], phi0.at[p0(FIRST + i), pl.ds(0, TILES)], local_sem.at[i]) for i in range(OWN)
    ]
    for i in (0, 3, 1, 2):
        loads[i].start()

    barrier = pltpu.get_barrier_semaphore()
    for where in (to_low, to_high, to_partner):
        pl.semaphore_signal(barrier, inc=1, device_id=where, device_id_type=mesh_id)
    pl.semaphore_wait(barrier, 3)

    def part(ref, slot, first=0, number=TILES):
        return ref.at[slot, pl.ds(first, number)]

    def shift(ref, name, source, target, k, where, first=0, number=TILES):
        send, recv = (down_send, down_recv) if where is to_low else (up_send, up_recv)
        return remote(part(ref, name(source), first, number), part(ref, name(target), first, number),
                      send.at[k], recv.at[k], where)

    down = [
        shift(phi0, p0, 4, 8, 0, to_low), shift(phi0, p0, 5, 9, 1, to_low),
        shift(phi1, p1, 5, 9, 2, to_low), shift(phi1, p1, 4, 8, 3, to_low),
        shift(phi1, p1, 6, 10, 4, to_low, 2, 2), shift(phi1, p1, 6, 10, 5, to_low, 0, 2),
    ]
    up = [
        shift(phi0, p0, 7, 3, 0, to_high), shift(phi0, p0, 6, 2, 1, to_high),
        shift(phi1, p1, 6, 2, 2, to_high), shift(phi1, p1, 7, 3, 3, to_high),
        shift(phi1, p1, 5, 1, 4, to_high, 0, 2), shift(phi1, p1, 5, 1, 5, to_high, 2, 2),
    ]
    down_new = [
        [remote(phi2[t].at[p2(source)], phi2[t].at[p2(target)], new_send.at[k, t], new_recv.at[k, t], to_low)
         for t in range(TILES)]
        for k, (source, target) in enumerate(((5, 9), (6, 10)))
    ]
    up_new = [
        remote(phi2[t].at[p2(6)], phi2[t].at[p2(2)], new_send.at[2, t], new_recv.at[2, t], to_high)
        for t in range(TILES)
    ]

    row_moves = []

    def send_rows(ref, slot, rows):
        copies = []
        for k, tile in enumerate((0, TILES - 1)):
            n = len(row_moves)
            copy = remote(ref.at[slot, tile], rows.at[slot, k], row_send.at[n], row_recv.at[n], to_partner)
            copy.start()
            row_moves.append(copy)
            copies.append(copy)
        return copies

    def halo(ref, slot, rows, copies):
        for copy in copies:
            copy.wait_recv()
        for c in chunks:
            ref[slot, TILES, :, c : c + half] = jnp.where(
                sub < SUB // 2, rows[slot, 0, :, c : c + half], rows[slot, 1, :, c : c + half]
            )

    sub = lax.broadcasted_iota(jnp.int32, (SUB, half), 0)
    chunks = range(0, cols, half)

    for i in (0, 3, 1, 2):
        loads[i].wait()
        if i == 0:
            down[0].start()
        elif i == 3:
            up[0].start()
        elif i == 1:
            down[1].start()
        else:
            up[1].start()
    own_rows = [send_rows(phi0, p0(image), rows0) for image in range(FIRST, FIRST + OWN)]
    far = 1
    step = 0
    lives = []
    while 2 * far < count + 1 and far < count // 2:
        lives.append(far)
        far *= 2

    def say_live(step):
        distance = lives[step]
        for other in (lax.rem(img + distance, count), lax.rem(img + count - distance, count)):
            pl.semaphore_signal(live.at[step], inc=1, device_id={"img": other}, device_id_type=mesh_id)

    def hear_live(step):
        pl.semaphore_wait(live.at[step], 2)

    if lives:
        say_live(0)

    is_first = (img == 0).astype(jnp.int32)
    is_last = (img == count - 1).astype(jnp.int32)
    last = OWN * count - 1

    def same(image, k):
        return jnp.asarray(image == k).astype(jnp.int32)

    def sides(image):
        at_first = is_first * same(image, FIRST)
        at_last = is_last * same(image, FIRST + OWN - 1)
        end = (at_first + at_last).astype(jnp.float32)
        return image - 1 + at_first, image + 1 - at_last, (1.0 + end) * jnp.float32(last / 2.0)

    def around(ref, slot, tile, c):
        above = lax.rem(tile + EXT - 1, EXT)
        below = lax.rem(tile + 1, EXT)
        here = ref[slot, tile, :, c : c + half]
        up_rows = pltpu.roll(jnp.where(sub == SUB - 1, ref[slot, above, :, c : c + half], here), 1, 0)
        down_rows = pltpu.roll(jnp.where(sub == 0, ref[slot, below, :, c : c + half], here), SUB - 1, 0)
        if half == cols:
            left = pltpu.roll(here, 1, 1)
            right = pltpu.roll(here, half - 1, 1)
        else:
            before = (c - LANES) % cols
            after = (c + half) % cols
            wide = jnp.concatenate(
                [ref[slot, tile, :, before : before + LANES], here, ref[slot, tile, :, after : after + LANES]], axis=1
            )
            left = pltpu.roll(wide, 1, 1)[:, LANES : LANES + half]
            right = pltpu.roll(wide, half + 2 * LANES - 1, 1)[:, LANES : LANES + half]
        return here, (up_rows + down_rows) + (left + right) - 4.0 * here

    zero = jnp.zeros((SUB, LANES), jnp.float32)

    def over(tiles, one, init):
        first, end = tiles
        return lax.fori_loop(first, end, one, init)

    full, slab, upper_half, lower_half = (0, EXT), (0, TILES), (0, 2), (2, TILES)

    def drift(phi, th, slot, th_slot, tiles, total=None):
        def one(tile, acc):
            for c in chunks:
                here, lap = around(phi, slot, tile, c)
                force = lap + here - here * here * here
                th[th_slot, tile, :, c : c + half] = force
                acc = acc + jnp.where(tile < TILES, fold(force * force), 0.0)
            return acc

        acc = over(tiles, one, zero)
        if total is not None:
            total[...] = acc

    def stretch_sum(phi, lower, upper, total, factor):
        def one(tile, acc):
            for c in chunks:
                gap = phi[upper, tile, :, c : c + half] - phi[lower, tile, :, c : c + half]
                acc = acc + fold(gap * gap)
            return acc

        total[...] = over(slab, one, zero) * (factor * factor)

    def segment_sum(image, total, tiles=range(TILES)):
        acc = zero
        for t in tiles:
            for c in chunks:
                gap = phi2[t][p2(image), :, c : c + half] - phi2[t][p2(image - 1), :, c : c + half]
                acc = acc + fold(gap * gap)
        total[...] = acc

    def theta(phi, th, lower, upper, factor, th_slot, speed, tiles):
        scale = spread(speed * factor, half)

        def one(tile, carry):
            for c in chunks:
                span = slice(c, c + half)
                gap = phi[upper, tile, :, span] - phi[lower, tile, :, span]
                th[th_slot, tile, :, span] = scale * gap - th[th_slot, tile, :, span]
            return carry

        over(tiles, one, 0)

    def advance(phi, slot, th, th_slot, new, new_slot, speed, image, tiles):
        fixed = is_first * same(image, FIRST) + is_last * same(image, FIRST + OWN - 1)
        scale = spread(speed * jnp.float32(last / 2.0), half)

        def one(tile, carry):
            for c in chunks:
                span = slice(c, c + half)
                here, lap = around(th, th_slot, tile, c)
                old = phi[slot, tile, :, span]
                bend = th[th_slot + 1, tile, :, span] - th[th_slot - 1, tile, :, span]
                descent = scale * bend + lap + (1.0 - 3.0 * old * old) * here
                value = jnp.where(fixed == 0, old + TIME_STEP * descent, old)
                if new is phi2:
                    new[tile][new_slot, :, span] = value
                else:
                    new[new_slot, tile, :, span] = value
            return carry

        if new is phi2:
            for tile in range(*tiles):
                one(tile, 0)
        else:
            over(tiles, one, 0)

    def whole(a):
        return jnp.broadcast_to(jnp.sum(jnp.sum(a, axis=1, keepdims=True), axis=0, keepdims=True), (SUB, LANES))

    def speeds(mine, theirs, first, number, out_ref):
        for i in range(first, first + number):
            force = whole(mine[i, 0] + theirs[i, 0])
            stretch = whole(mine[i, 1] + theirs[i, 1])
            out_ref[i] = jnp.sqrt(force + EPSILON) / jnp.sqrt(stretch + EPSILON)

    def place(image):
        if isinstance(image, int):
            return 2 * (5 - image) if image < 6 else 2 * (image - 6) + 1
        return jnp.where(image < 6, 2 * (5 - image), 2 * (image - 6) + 1)

    def each(images, body):
        start, step, number = images

        def one(i, carry):
            body(start + step * i)
            return carry

        lax.fori_loop(0, number, one, 0)

    every, mids, ends, outs = (4, 1, 4), (5, 1, 2), (4, 3, 2), (3, 5, 2)

    def gap0(image):
        lower, upper, factor = sides(image)
        stretch_sum(phi0, p0(lower), p0(upper), mine0.at[place(image), 1], factor)

    def drift0(image):
        drift(phi0, th0, p0(image), t0(image), full, mine0.at[place(image), 0])

    def theta0(image):
        lower, upper, factor = sides(image)
        theta(phi0, th0, p0(lower), p0(upper), factor, t0(image), speed0[place(image)], full)

    def next1(image):
        advance(phi0, p0(image), th0, t0(image), phi1, p1(image), speed0[place(image)], image, full)

    def gap1(image):
        lower, upper, factor = sides(image)
        stretch_sum(phi1, p1(lower), p1(upper), mine1.at[place(image), 1], factor)

    def drift1(image):
        drift(phi1, th1, p1(image), t1(image), full, mine1.at[place(image), 0])

    def theta1(image, tiles=full):
        lower, upper, factor = sides(image)
        theta(phi1, th1, p1(lower), p1(upper), factor, t1(image), speed1[place(image)], tiles)

    def next2(image, tiles=slab):
        advance(phi1, p1(image), th1, t1(image), phi2, p2(image), speed1[place(image)], image, tiles)

    swaps = []

    def exchange(mine, theirs, first, number):
        k = len(swaps)
        span = pl.ds(first, number)
        move = remote(mine.at[span], theirs.at[span], sum_send.at[k], sum_recv.at[k], to_partner)
        move.start()
        swaps.append(move)
        return move

    def arrive(k):
        down[k].wait_recv()
        up[k].wait_recv()

    def live_round(n):
        if n < len(lives):
            hear_live(n)
            if n + 1 < len(lives):
                say_live(n + 1)

    for image in range(FIRST, FIRST + OWN):
        halo(phi0, p0(image), rows0, own_rows[image - FIRST])
    each(every, drift0)
    each(mids, gap0)

    arrive(0)
    rows = {image: send_rows(phi0, p0(image), rows0) for image in (3, 8)}
    each(ends, gap0)
    move = exchange(mine0, theirs0, 0, OWN)
    for image in (3, 8):
        halo(phi0, p0(image), rows0, rows[image])
    move.wait_recv()
    speeds(mine0, theirs0, 0, OWN, speed0)
    each(every, theta0)
    each(mids, next1)
    down[2].start()
    up[2].start()
    each(outs, drift0)
    each(mids, drift1)
    live_round(0)

    arrive(1)
    rows = {image: send_rows(phi0, p0(image), rows0) for image in (2, 9)}
    each(outs, gap0)
    move = exchange(mine0, theirs0, OWN, 2)
    for image in (2, 9):
        halo(phi0, p0(image), rows0, rows[image])
    move.wait_recv()
    speeds(mine0, theirs0, OWN, 2, speed0)
    each(outs, theta0)
    each(ends, next1)
    down[3].start()
    up[3].start()
    each(mids, gap1)
    move = exchange(mine1, theirs1, 0, 2)
    each(ends, drift1)
    move.wait_recv()
    speeds(mine1, theirs1, 0, 2, speed1)
    paces = [
        remote(speed1.at[0], speed1.at[7], pace_send.at[0], pace_recv.at[0], to_low),
        remote(speed1.at[1], speed1.at[6], pace_send.at[1], pace_recv.at[1], to_high),
    ]
    each(mids, theta1)
    for copy in paces + down[4:6] + up[4:6]:
        copy.start()
    live_round(1)

    arrive(2)
    rows = {image: send_rows(phi1, p1(image), rows1) for image in (2, 9)}
    each(outs, gap1)
    for image in (2, 9):
        halo(phi1, p1(image), rows1, rows[image])
    for image in (2, 9):
        drift(phi1, th1, p1(image), t1(image), slab)
    live_round(2)

    arrive(3)
    rows = {image: send_rows(phi1, p1(image), rows1) for image in (3, 8)}
    each(ends, gap1)
    move = exchange(mine1, theirs1, 2, 2)
    for image in (3, 8):
        halo(phi1, p1(image), rows1, rows[image])
    each(outs, drift1)
    last_move = exchange(mine1, theirs1, 4, 2)
    move.wait_recv()
    speeds(mine1, theirs1, 2, 2, speed1)
    each(ends, theta1)
    each(mids, next2)
    last_move.wait_recv()
    speeds(mine1, theirs1, 4, 2, speed1)
    each(outs, theta1)
    each(ends, next2)
    for image in (5, 6, 7):
        segment_sum(image, mine2.at[image - FIRST])
    live_round(3)

    for copy in paces:
        copy.wait_recv()
    arrive(4)

    def cross(low_tiles, high_tiles):
        theta1(2, low_tiles)
        theta1(9, high_tiles)
        next2(3, low_tiles)
        next2(8, high_tiles)

    cross(upper_half, lower_half)
    segment_sum(4, mine2.at[0], range(*upper_half))
    segment_sum(8, mine2.at[OWN], range(*lower_half))
    move = exchange(mine2, theirs2, 0, OWN + 1)
    move.wait_recv()

    lane = lax.broadcasted_iota(jnp.int32, (1, LANES), 1)
    squares = jnp.zeros((1, LANES), jnp.float32)
    for i in range(OWN + 1):
        squares = jnp.where(lane == i, whole(mine2[i] + theirs2[i])[0:1], squares)
    message[0] = squares
    gathered[img] = squares

    def send_length(k):
        return remote(message.at[0], gathered.at[img], len_send.at[k], len_recv.at[k], {"img": lax.rem(img + k, count)})

    def spread_out(i, carry):
        distance = count // 2 - 1 - i
        send_length(distance).start()
        send_length(count - distance).start()
        return carry

    send_length(count // 2).start()
    lax.fori_loop(0, count // 2 - 1, spread_out, 0)
    for group in down_new + [up_new]:
        for copy in group:
            copy.start()
    arrive(5)
    cross(lower_half, upper_half)

    def heard(k, carry):
        send_length(k).wait_recv()
        return carry

    lax.fori_loop(1, count, heard, 0)

    owner = lax.broadcasted_iota(jnp.int32, (count, 1, LANES), 0)
    spot = lax.broadcasted_iota(jnp.int32, (count, 1, LANES), 2)
    index = OWN * owner + spot
    squares = gathered[...]
    before = jnp.concatenate([squares[count - 1 :], squares[: count - 1]], axis=0)
    halves = jnp.where(spot == 0, squares, 0.0) + jnp.where(spot == OWN, before, 0.0)
    squares = jnp.where(spot == 0, jnp.sum(halves, axis=2, keepdims=True), squares)
    segs = jnp.where((spot < OWN) & (index > 0), jnp.sqrt(squares + EPSILON), 0.0)

    def add_up(a):
        return jnp.sum(jnp.sum(a, axis=0), axis=1, keepdims=True)

    length = add_up(segs)
    weights = []
    for i in range(OWN):
        base = bracket[i]
        arc = add_up(jnp.where(index <= base, segs, 0.0))
        seg = add_up(jnp.where(index == base + 1, segs, 0.0))
        target = length * (OWN * img + i).astype(jnp.float32) / jnp.float32(last)
        weights.append(jnp.broadcast_to((target - arc) / seg, (SUB, half)))

    writes = [pltpu.make_async_copy(result.at[t], out.at[t], out_sem.at[t]) for t in range(TILES)]
    for t in range(TILES):
        for group in down_new + [up_new]:
            group[t].wait_recv()
        for i in range(OWN):
            pick = jnp.clip(bracket[i] - (OWN * img - 2), 0, 7)
            for c in chunks:
                span = slice(c, c + half)
                base = phi2[t][pick, :, span]
                result[t, i, :, span] = base + weights[i] * (phi2[t][pick + 1, :, span] - base)
        writes[t].start()

    for copy in down + up + row_moves + swaps + paces + up_new + down_new[0] + down_new[1]:
        copy.wait_send()

    def sent(k, carry):
        send_length(k).wait_send()
        return carry

    lax.fori_loop(1, count, sent, 0)
    for copy in writes:
        copy.wait()


def per_device(count, path, bracket):
    images, rows, cols = path.shape
    f32 = jnp.float32
    dma = pltpu.SemaphoreType.DMA
    tiled = path.reshape(images, TILES, SUB, cols)

    def slabs(number, tiles=EXT):
        return pltpu.VMEM((number, tiles, SUB, cols), f32)

    def small(*dims):
        return pltpu.VMEM((*dims, SUB, LANES), f32)

    out = pl.pallas_call(
        functools.partial(kernel, count),
        out_shape=jax.ShapeDtypeStruct((TILES, images, SUB, cols), f32),
        in_specs=[pl.BlockSpec(memory_space=pl.ANY), pl.BlockSpec(memory_space=pltpu.SMEM)],
        out_specs=pl.BlockSpec(memory_space=pl.ANY),
        scratch_shapes=[
            slabs(8),
            slabs(10),
            *[pltpu.VMEM((9, SUB, cols), f32) for _ in range(TILES)],
            slabs(6),
            slabs(8),
            slabs(8, 2),
            slabs(10, 2),
            small(6, 2), small(6, 2),
            small(6, 2), small(6, 2),
            small(OWN + 1), small(OWN + 1),
            small(6), small(8),
            pltpu.VMEM((1, 1, LANES), f32),
            pltpu.VMEM((count, 1, LANES), f32),
            pltpu.VMEM((TILES, images, SUB, cols), f32),
            dma((OWN,)),
            dma((6,)), dma((6,)), dma((6,)), dma((6,)),
            dma((24,)), dma((24,)),
            dma((8,)), dma((8,)),
            dma((3, TILES)), dma((3, TILES)),
            dma((2,)), dma((2,)),
            dma((count,)), dma((count,)),
            dma((TILES,)),
            pltpu.SemaphoreType.REGULAR((8,)),
        ],
        compiler_params=pltpu.CompilerParams(
            collective_id=0, has_side_effects=True, vmem_limit_bytes=60 * 1024 * 1024
        ),
    )(tiled, bracket)
    return out.transpose(1, 0, 2, 3).reshape(images, rows, cols)


def solution(mesh):
    count = mesh.shape["img"]
    return jax.shard_map(
        functools.partial(per_device, count),
        mesh=mesh,
        in_specs=(P(("groups", "img"), "space", None), P(("groups", "img"))),
        out_specs=P(("groups", "img"), "space", None),
        check_vma=False,
    )
```

time: 115 us -> 111 us (0.965)
  Pallas kernels: 111 us -> 107 us
    pallas_call x1, Pallas kernels: 111 us -> 107 us  [per_device(): pl.pallas_call(functools.partial(kernel, count), out_shape=jax.ShapeDtype...]
where the time goes in v2:
time: 111 us; the launch traced here: 110 us
  Pallas kernels  107 us (96%)
  local copies, waits for them, and re-layouts  3.11 us (3%)
    pallas_call x1, Pallas kernels, per_device(): pl.pallas_call(functools.partial(kernel, count), out_shape=jax.ShapeDtype...  107 us
    reshape x1, local copies, waits for them, and re-layouts, per_device(): return out.transpose(1, 0, 2, 3).reshape(images, rows, cols)  3.11 us

profile of v2, /device:TPU:37, one launch (start us, length us, event | category | flops | bytes accessed | tf_op | source)
XLA Modules:
  0.0 110.5 jit_solution(9092184898557218760)
XLA Ops:
  0.0 107.3 %shard_map.28 = f32[4,4,8,4096]{3,2,1,0:T(8,128)} custom-call(f32[4,4,8,4096]{3,2,1,0:T(8,128)} %bitcast.6, s32[4]{0:T(128)} %bracket.1), custom_call_target="tpu_custom_call" | custom-call | tf_op jit(solution)/shard_map/pallas_call | solution.py:506
  107.3 3.1 %copy_bitcast_fusion = f32[4,32,4096]{2,1,0:T(8,128)} fusion(f32[4,4,8,4096]{3,2,1,0:T(8,128)} %shard_map.28), kind=kLoop, calls=%fused_computation | loop fusion | bytes 4194304 | tf_op jit(solution)/shard_map/reshape | solution.py:540

commit v3 on v2

--- a/solution.py
+++ b/solution.py
@@ -61,9 +61,20 @@
         loads[i].start()
 
     barrier = pltpu.get_barrier_semaphore()
-    for where in (to_low, to_high, to_partner):
-        pl.semaphore_signal(barrier, inc=1, device_id=where, device_id_type=mesh_id)
-    pl.semaphore_wait(barrier, 3)
+    def signal(sem, where):
+        pl.semaphore_signal(sem, inc=1, device_id=where, device_id_type=mesh_id)
+
+    has_low, has_high = img > 0, img < count - 1
+    pl.when(has_low)(lambda: signal(barrier, to_low))
+    pl.when(has_high)(lambda: signal(barrier, to_high))
+    signal(barrier, to_partner)
+    pl.semaphore_wait(barrier, 1 + has_low.astype(jnp.int32) + has_high.astype(jnp.int32))
+
+    def when(condition, copies, act):
+        @pl.when(condition)
+        def _():
+            for copy in copies:
+                getattr(copy, act)()
 
     def part(ref, slot, first=0, number=TILES):
         return ref.at[slot, pl.ds(first, number)]
@@ -93,6 +104,12 @@
         for t in range(TILES)
     ]
 
+    def go_down(*copies):
+        when(has_low, copies, "start")
+
+    def go_up(*copies):
+        when(has_high, copies, "start")
+
     row_moves = []
 
     def send_rows(ref, slot, rows):
@@ -118,29 +135,22 @@
 
     for i in (0, 3, 1, 2):
         loads[i].wait()
-        if i == 0:
-            down[0].start()
-        elif i == 3:
-            up[0].start()
-        elif i == 1:
-            down[1].start()
+        if i < 2:
+            go_down(down[i])
         else:
-            up[1].start()
+            go_up(up[3 - i])
     own_rows = [send_rows(phi0, p0(image), rows0) for image in range(FIRST, FIRST + OWN)]
-    far = 1
-    step = 0
     lives = []
-    while 2 * far < count + 1 and far < count // 2:
-        lives.append(far)
-        far *= 2
-
-    def say_live(step):
-        distance = lives[step]
-        for other in (lax.rem(img + distance, count), lax.rem(img + count - distance, count)):
-            pl.semaphore_signal(live.at[step], inc=1, device_id={"img": other}, device_id_type=mesh_id)
-
-    def hear_live(step):
-        pl.semaphore_wait(live.at[step], 2)
+    while 2 ** len(lives) < count - 1:
+        lives.append(2 ** len(lives))
+
+    def say_live(n):
+        for where in (img - lives[n], img + lives[n]):
+            pl.when((where >= 0) & (where < count))(lambda where=where: signal(live.at[n], {"img": where}))
+
+    def hear_live(n):
+        below, above = img >= lives[n], img < count - lives[n]
+        pl.semaphore_wait(live.at[n], below.astype(jnp.int32) + above.astype(jnp.int32))
 
     if lives:
         say_live(0)
@@ -315,8 +325,8 @@
         return move
 
     def arrive(k):
-        down[k].wait_recv()
-        up[k].wait_recv()
+        when(has_high, [down[k]], "wait_recv")
+        when(has_low, [up[k]], "wait_recv")
 
     def live_round(n):
         if n < len(lives):
@@ -326,8 +336,10 @@
 
     for image in range(FIRST, FIRST + OWN):
         halo(phi0, p0(image), rows0, own_rows[image - FIRST])
+    live_round(0)
     each(every, drift0)
     each(mids, gap0)
+    live_round(1)
 
     arrive(0)
     rows = {image: send_rows(phi0, p0(image), rows0) for image in (3, 8)}
@@ -339,11 +351,11 @@
     speeds(mine0, theirs0, 0, OWN, speed0)
     each(every, theta0)
     each(mids, next1)
-    down[2].start()
-    up[2].start()
+    go_down(down[2])
+    go_up(up[2])
     each(outs, drift0)
     each(mids, drift1)
-    live_round(0)
+    live_round(2)
 
     arrive(1)
     rows = {image: send_rows(phi0, p0(image), rows0) for image in (2, 9)}
@@ -355,8 +367,8 @@
     speeds(mine0, theirs0, OWN, 2, speed0)
     each(outs, theta0)
     each(ends, next1)
-    down[3].start()
-    up[3].start()
+    go_down(down[3])
+    go_up(up[3])
     each(mids, gap1)
     move = exchange(mine1, theirs1, 0, 2)
     each(ends, drift1)
@@ -367,9 +379,9 @@
         remote(speed1.at[1], speed1.at[6], pace_send.at[1], pace_recv.at[1], to_high),
     ]
     each(mids, theta1)
-    for copy in paces + down[4:6] + up[4:6]:
-        copy.start()
-    live_round(1)
+    go_down(paces[0], *down[4:6])
+    go_up(paces[1], *up[4:6])
+    live_round(3)
 
     arrive(2)
     rows = {image: send_rows(phi1, p1(image), rows1) for image in (2, 9)}
@@ -378,7 +390,6 @@
         halo(phi1, p1(image), rows1, rows[image])
     for image in (2, 9):
         drift(phi1, th1, p1(image), t1(image), slab)
-    live_round(2)
 
     arrive(3)
     rows = {image: send_rows(phi1, p1(image), rows1) for image in (3, 8)}
@@ -398,10 +409,9 @@
     each(ends, next2)
     for image in (5, 6, 7):
         segment_sum(image, mine2.at[image - FIRST])
-    live_round(3)
-
-    for copy in paces:
-        copy.wait_recv()
+
+    when(has_high, [paces[0]], "wait_recv")
+    when(has_low, [paces[1]], "wait_recv")
     arrive(4)
 
     def cross(low_tiles, high_tiles):
@@ -423,6 +433,8 @@
     message[0] = squares
     gathered[img] = squares
 
+    live_round(4)
+
     def send_length(k):
         return remote(message.at[0], gathered.at[img], len_send.at[k], len_recv.at[k], {"img": lax.rem(img + k, count)})
 
@@ -434,9 +446,8 @@
 
     send_length(count // 2).start()
     lax.fori_loop(0, count // 2 - 1, spread_out, 0)
-    for group in down_new + [up_new]:
-        for copy in group:
-            copy.start()
+    go_down(*down_new[0], *down_new[1])
+    go_up(*up_new)
     arrive(5)
     cross(lower_half, upper_half)
 
@@ -467,10 +478,10 @@
         target = length * (OWN * img + i).astype(jnp.float32) / jnp.float32(last)
         weights.append(jnp.broadcast_to((target - arc) / seg, (SUB, half)))
 
-    writes = [pltpu.make_async_copy(result.at[t], out.at[t], out_sem.at[t]) for t in range(TILES)]
+    writes = [pltpu.make_async_copy(result.at[t], out.at[pl.ds(0, OWN), t], out_sem.at[t]) for t in range(TILES)]
     for t in range(TILES):
-        for group in down_new + [up_new]:
-            group[t].wait_recv()
+        when(has_high, [down_new[0][t], down_new[1][t]], "wait_recv")
+        when(has_low, [up_new[t]], "wait_recv")
         for i in range(OWN):
             pick = jnp.clip(bracket[i] - (OWN * img - 2), 0, 7)
             for c in chunks:
@@ -479,7 +490,9 @@
                 result[t, i, :, span] = base + weights[i] * (phi2[t][pick + 1, :, span] - base)
         writes[t].start()
 
-    for copy in down + up + row_moves + swaps + paces + up_new + down_new[0] + down_new[1]:
+    when(has_low, down + down_new[0] + down_new[1] + paces[:1], "wait_send")
+    when(has_high, up + up_new + paces[1:], "wait_send")
+    for copy in row_moves + swaps:
         copy.wait_send()
 
     def sent(k, carry):
@@ -505,7 +518,7 @@
 
     out = pl.pallas_call(
         functools.partial(kernel, count),
-        out_shape=jax.ShapeDtypeStruct((TILES, images, SUB, cols), f32),
+        out_shape=jax.ShapeDtypeStruct((images, TILES, SUB, cols), f32),
         in_specs=[pl.BlockSpec(memory_space=pl.ANY), pl.BlockSpec(memory_space=pltpu.SMEM)],
         out_specs=pl.BlockSpec(memory_space=pl.ANY),
         scratch_shapes=[
@@ -537,7 +550,7 @@
             collective_id=0, has_side_effects=True, vmem_limit_bytes=60 * 1024 * 1024
         ),
     )(tiled, bracket)
-    return out.transpose(1, 0, 2, 3).reshape(images, rows, cols)
+    return out.reshape(images, rows, cols)
 
 
 def solution(mesh):

time: 111 us -> 108 us (0.973)
  Pallas kernels: 107 us -> 104 us
    reshape x1 -> x0, local copies, waits for them, and re-layouts: 3.11 us -> none  [per_device(): return out.transpose(1, 0, 2, 3).reshape(images, rows, cols)]
    unnamed x0 -> x1, local copies, waits for them, and re-layouts: none -> 3.11 us
    pallas_call x1, Pallas kernels: 107 us -> 104 us  [per_device(): pl.pallas_call(functools.partial(kernel, count), out_shape=jax.ShapeDtype...]
where the time goes in v3:
time: 108 us
  Pallas kernels  104 us (96%)
  local copies, waits for them, and re-layouts  3.11 us (3%)
    pallas_call x1, Pallas kernels, per_device(): pl.pallas_call(functools.partial(kernel, count), out_shape=jax.ShapeDtype...  104 us
    unnamed x1, local copies, waits for them, and re-layouts  3.11 us

profile of v3, /device:TPU:37, one launch (start us, length us, event | category | flops | bytes accessed | tf_op | source)
XLA Modules:
  0.0 107.6 jit_solution(6905379894215116314)
XLA Ops:
  0.0 104.5 %shard_map.28 = f32[4,4,8,4096]{3,2,1,0:T(8,128)} custom-call(f32[4,4,8,4096]{3,2,1,0:T(8,128)} %bitcast.3, s32[4]{0:T(128)} %bracket.1), custom_call_target="tpu_custom_call" | custom-call | tf_op jit(solution)/shard_map/pallas_call | solution.py:519
  104.5 3.1 %copy.4 = f32[4,32,4096]{2,1,0:T(8,128)} copy(f32[4,32,4096]{2,1,0:T(8,128)} %bitcast.2) | data formatting | bytes 4194304

commit v4 on v3

--- a/solution.py
+++ b/solution.py
@@ -31,10 +31,10 @@
     return jnp.concatenate([vector] * (width // LANES), axis=1)
 
 
-def kernel(count, path, bracket, out, phi0, phi1, phi2_0, phi2_1, phi2_2, phi2_3, th0, th1, rows0, rows1,
-           mine0, theirs0, mine1, theirs1, mine2, theirs2, speed0, speed1, message, gathered, result,
+def kernel(count, path, given, out, phi0, phi1, phi2_0, phi2_1, phi2_2, phi2_3, th0, th1, rows0, rows1,
+           mine0, theirs0, mine1, theirs1, mine2, theirs2, speed0, speed1, message, gathered, lengths,
            local_sem, down_send, down_recv, up_send, up_recv, row_send, row_recv, sum_send, sum_recv,
-           new_send, new_recv, pace_send, pace_recv, len_send, len_recv, out_sem, live):
+           new_send, new_recv, pace_send, pace_recv, len_send, len_recv, bracket, given_sem, live):
     cols = path.shape[-1]
     half = min(cols, 1024)
     phi2 = (phi2_0, phi2_1, phi2_2, phi2_3)
@@ -59,6 +59,8 @@
     ]
     for i in (0, 3, 1, 2):
         loads[i].start()
+    given_load = pltpu.make_async_copy(given, bracket, given_sem)
+    given_load.start()
 
     barrier = pltpu.get_barrier_semaphore()
     def signal(sem, where):
@@ -67,8 +69,9 @@
     has_low, has_high = img > 0, img < count - 1
     pl.when(has_low)(lambda: signal(barrier, to_low))
     pl.when(has_high)(lambda: signal(barrier, to_high))
+    neighbours = has_low.astype(jnp.int32) + has_high.astype(jnp.int32)
+    pl.semaphore_wait(barrier, neighbours + (1 - core))
     signal(barrier, to_partner)
-    pl.semaphore_wait(barrier, 1 + has_low.astype(jnp.int32) + has_high.astype(jnp.int32))
 
     def when(condition, copies, act):
         @pl.when(condition)
@@ -139,6 +142,7 @@
             go_down(down[i])
         else:
             go_up(up[3 - i])
+    pl.when(core == 1)(lambda: pl.semaphore_wait(barrier, 1))
     own_rows = [send_rows(phi0, p0(image), rows0) for image in range(FIRST, FIRST + OWN)]
     lives = []
     while 2 ** len(lives) < count - 1:
@@ -444,23 +448,40 @@
         send_length(count - distance).start()
         return carry
 
-    send_length(count // 2).start()
-    lax.fori_loop(0, count // 2 - 1, spread_out, 0)
+    @pl.when(core == 1)
+    def _():
+        send_length(count // 2).start()
+        lax.fori_loop(0, count // 2 - 1, spread_out, 0)
+
     go_down(*down_new[0], *down_new[1])
     go_up(*up_new)
     arrive(5)
     cross(lower_half, upper_half)
 
+    when(has_low, down + paces[:1], "wait_send")
+    when(has_high, up + paces[1:], "wait_send")
+    for copy in row_moves + swaps:
+        copy.wait_send()
+
     def heard(k, carry):
+        send_length(k).wait_send()
         send_length(k).wait_recv()
         return carry
 
-    lax.fori_loop(1, count, heard, 0)
+    hand_over = remote(gathered, lengths, sum_send.at[7], sum_recv.at[7], to_partner)
+
+    @pl.when(core == 1)
+    def _():
+        lax.fori_loop(1, count, heard, 0)
+        hand_over.start()
+        lengths[...] = gathered[...]
+
+    pl.when(core == 0)(hand_over.wait_recv)
 
     owner = lax.broadcasted_iota(jnp.int32, (count, 1, LANES), 0)
     spot = lax.broadcasted_iota(jnp.int32, (count, 1, LANES), 2)
     index = OWN * owner + spot
-    squares = gathered[...]
+    squares = lengths[...]
     before = jnp.concatenate([squares[count - 1 :], squares[: count - 1]], axis=0)
     halves = jnp.where(spot == 0, squares, 0.0) + jnp.where(spot == OWN, before, 0.0)
     squares = jnp.where(spot == 0, jnp.sum(halves, axis=2, keepdims=True), squares)
@@ -469,6 +490,7 @@
     def add_up(a):
         return jnp.sum(jnp.sum(a, axis=0), axis=1, keepdims=True)
 
+    given_load.wait()
     length = add_up(segs)
     weights = []
     for i in range(OWN):
@@ -478,7 +500,6 @@
         target = length * (OWN * img + i).astype(jnp.float32) / jnp.float32(last)
         weights.append(jnp.broadcast_to((target - arc) / seg, (SUB, half)))
 
-    writes = [pltpu.make_async_copy(result.at[t], out.at[pl.ds(0, OWN), t], out_sem.at[t]) for t in range(TILES)]
     for t in range(TILES):
         when(has_high, [down_new[0][t], down_new[1][t]], "wait_recv")
         when(has_low, [up_new[t]], "wait_recv")
@@ -487,21 +508,11 @@
             for c in chunks:
                 span = slice(c, c + half)
                 base = phi2[t][pick, :, span]
-                result[t, i, :, span] = base + weights[i] * (phi2[t][pick + 1, :, span] - base)
-        writes[t].start()
-
-    when(has_low, down + down_new[0] + down_new[1] + paces[:1], "wait_send")
-    when(has_high, up + up_new + paces[1:], "wait_send")
-    for copy in row_moves + swaps:
-        copy.wait_send()
-
-    def sent(k, carry):
-        send_length(k).wait_send()
-        return carry
-
-    lax.fori_loop(1, count, sent, 0)
-    for copy in writes:
-        copy.wait()
+                out[i, t, :, span] = base + weights[i] * (phi2[t][pick + 1, :, span] - base)
+
+    when(has_low, down_new[0] + down_new[1], "wait_send")
+    when(has_high, up_new, "wait_send")
+    pl.when(core == 1)(hand_over.wait_send)
 
 
 def per_device(count, path, bracket):
@@ -519,8 +530,8 @@
     out = pl.pallas_call(
         functools.partial(kernel, count),
         out_shape=jax.ShapeDtypeStruct((images, TILES, SUB, cols), f32),
-        in_specs=[pl.BlockSpec(memory_space=pl.ANY), pl.BlockSpec(memory_space=pltpu.SMEM)],
-        out_specs=pl.BlockSpec(memory_space=pl.ANY),
+        in_specs=[pl.BlockSpec(memory_space=pltpu.HBM), pl.BlockSpec(memory_space=pltpu.HBM)],
+        out_specs=pl.BlockSpec(memory_space=pltpu.VMEM),
         scratch_shapes=[
             slabs(8),
             slabs(10),
@@ -535,7 +546,7 @@
             small(6), small(8),
             pltpu.VMEM((1, 1, LANES), f32),
             pltpu.VMEM((count, 1, LANES), f32),
-            pltpu.VMEM((TILES, images, SUB, cols), f32),
+            pltpu.VMEM((count, 1, LANES), f32),
             dma((OWN,)),
             dma((6,)), dma((6,)), dma((6,)), dma((6,)),
             dma((24,)), dma((24,)),
@@ -543,13 +554,13 @@
             dma((3, TILES)), dma((3, TILES)),
             dma((2,)), dma((2,)),
             dma((count,)), dma((count,)),
-            dma((TILES,)),
+            pltpu.SMEM((images,), jnp.int32), dma,
             pltpu.SemaphoreType.REGULAR((8,)),
         ],
         compiler_params=pltpu.CompilerParams(
-            collective_id=0, has_side_effects=True, vmem_limit_bytes=60 * 1024 * 1024
+            collective_id=0, has_side_effects=True, vmem_limit_bytes=40 * 1024 * 1024
         ),
-    )(tiled, bracket)
+    )(*(pltpu.with_memory_space_constraint(a, pltpu.HBM) for a in (tiled, bracket)))
     return out.reshape(images, rows, cols)
 
 

time: 108 us -> 94.7 us (0.88)
  Pallas kernels: 104 us -> 93.3 us
  local copies, waits for them, and re-layouts: 3.11 us -> 1.32 us
    pallas_call x1, Pallas kernels: 104 us -> 93.3 us  [per_device(): pl.pallas_call(functools.partial(kernel, count), out_shape=jax.ShapeDtype...]
    unnamed x1, local copies, waits for them, and re-layouts: 3.11 us -> 1.32 us
where the time goes in v4:
time: 94.7 us; the launch traced here: 94.6 us
  Pallas kernels  93.3 us (99%)
  local copies, waits for them, and re-layouts  1.32 us (1%)
    pallas_call x1, Pallas kernels, per_device(): pl.pallas_call(functools.partial(kernel, count), out_shape=jax.ShapeDtype...  93.3 us

profile of v4, /device:TPU:37, one launch (start us, length us, event | category | flops | bytes accessed | tf_op | source)
XLA Modules:
  0.0 94.6 jit_solution(17969316922147839176)
XLA Ops:
  0.0 93.3 %shard_map.28 = f32[4,4,8,4096]{3,2,1,0:T(8,128)S(1)} custom-call(f32[4,4,8,4096]{3,2,1,0:T(8,128)} %bitcast.3, s32[4]{0:T(128)} %given.1), custom_call_target="tpu_custom_call" | custom-call | tf_op jit(solution)/shard_map/pallas_call | solution.py:530
  93.3 1.3 %copy.4 = f32[4,32,4096]{2,1,0:T(8,128)} copy(f32[4,32,4096]{2,1,0:T(8,128)S(1)} %bitcast.2) | data formatting | bytes 4194304

commit v5 on v4

--- a/solution.py
+++ b/solution.py
@@ -33,8 +33,8 @@
 
 def kernel(count, path, given, out, phi0, phi1, phi2_0, phi2_1, phi2_2, phi2_3, th0, th1, rows0, rows1,
            mine0, theirs0, mine1, theirs1, mine2, theirs2, speed0, speed1, message, gathered, lengths,
-           local_sem, down_send, down_recv, up_send, up_recv, row_send, row_recv, sum_send, sum_recv,
-           new_send, new_recv, pace_send, pace_recv, len_send, len_recv, bracket, given_sem, live):
+           local_sem, side_send, down_recv, up_recv, row_send, row_recv, sum_send, sum_recv,
+           new_send, new_recv, pace_send, pace_recv, len_sem, bracket, given_sem, live):
     cols = path.shape[-1]
     half = min(cols, 1024)
     phi2 = (phi2_0, phi2_1, phi2_2, phi2_3)
@@ -51,6 +51,9 @@
         return pltpu.make_async_remote_copy(
             src_ref=src, dst_ref=dst, send_sem=send, recv_sem=recv, device_id=where, device_id_type=mesh_id
         )
+
+    def take(ref, sem):
+        remote(ref, ref, sem, sem, to_partner).wait_recv()
 
     p0, p1, p2, t0, t1 = (lambda w, s=s: w - s for s in (2, 1, 2, 3, 2))
 
@@ -83,9 +86,9 @@
         return ref.at[slot, pl.ds(first, number)]
 
     def shift(ref, name, source, target, k, where, first=0, number=TILES):
-        send, recv = (down_send, down_recv) if where is to_low else (up_send, up_recv)
+        send, recv = (side_send.at[0], down_recv) if where is to_low else (side_send.at[1], up_recv)
         return remote(part(ref, name(source), first, number), part(ref, name(target), first, number),
-                      send.at[k], recv.at[k], where)
+                      send, recv.at[k], where)
 
     down = [
         shift(phi0, p0, 4, 8, 0, to_low), shift(phi0, p0, 5, 9, 1, to_low),
@@ -98,12 +101,12 @@
         shift(phi1, p1, 5, 1, 4, to_high, 0, 2), shift(phi1, p1, 5, 1, 5, to_high, 2, 2),
     ]
     down_new = [
-        [remote(phi2[t].at[p2(source)], phi2[t].at[p2(target)], new_send.at[k, t], new_recv.at[k, t], to_low)
+        [remote(phi2[t].at[p2(source)], phi2[t].at[p2(target)], new_send.at[0], new_recv.at[0, t], to_low)
          for t in range(TILES)]
-        for k, (source, target) in enumerate(((5, 9), (6, 10)))
+        for source, target in ((5, 9), (6, 10))
     ]
     up_new = [
-        remote(phi2[t].at[p2(6)], phi2[t].at[p2(2)], new_send.at[2, t], new_recv.at[2, t], to_high)
+        remote(phi2[t].at[p2(6)], phi2[t].at[p2(2)], new_send.at[1], new_recv.at[1, t], to_high)
         for t in range(TILES)
     ]
 
@@ -113,25 +116,23 @@
     def go_up(*copies):
         when(has_high, copies, "start")
 
-    row_moves = []
-
-    def send_rows(ref, slot, rows):
-        copies = []
-        for k, tile in enumerate((0, TILES - 1)):
-            n = len(row_moves)
-            copy = remote(ref.at[slot, tile], rows.at[slot, k], row_send.at[n], row_recv.at[n], to_partner)
-            copy.start()
-            row_moves.append(copy)
-            copies.append(copy)
-        return copies
-
-    def halo(ref, slot, rows, copies):
-        for copy in copies:
-            copy.wait_recv()
-        for c in chunks:
-            ref[slot, TILES, :, c : c + half] = jnp.where(
-                sub < SUB // 2, rows[slot, 0, :, c : c + half], rows[slot, 1, :, c : c + half]
-            )
+    groups = []
+
+    def send_rows(ref, rows, slots):
+        n = len(groups)
+        groups.append(rows.at[pl.ds(0, len(slots))])
+        for slot in slots:
+            for k, tile in enumerate((0, TILES - 1)):
+                remote(ref.at[slot, tile], rows.at[slot, k], row_send.at[n], row_recv.at[n], to_partner).start()
+
+    def halos(ref, rows, slots):
+        n = len(groups) - 1
+        take(groups[n], row_recv.at[n])
+        for slot in slots:
+            for c in chunks:
+                ref[slot, TILES, :, c : c + half] = jnp.where(
+                    sub < SUB // 2, rows[slot, 0, :, c : c + half], rows[slot, 1, :, c : c + half]
+                )
 
     sub = lax.broadcasted_iota(jnp.int32, (SUB, half), 0)
     chunks = range(0, cols, half)
@@ -143,7 +144,8 @@
         else:
             go_up(up[3 - i])
     pl.when(core == 1)(lambda: pl.semaphore_wait(barrier, 1))
-    own_rows = [send_rows(phi0, p0(image), rows0) for image in range(FIRST, FIRST + OWN)]
+    own_slots = [p0(image) for image in range(FIRST, FIRST + OWN)]
+    send_rows(phi0, rows0, own_slots)
     lives = []
     while 2 ** len(lives) < count - 1:
         lives.append(2 ** len(lives))
@@ -338,19 +340,18 @@
             if n + 1 < len(lives):
                 say_live(n + 1)
 
-    for image in range(FIRST, FIRST + OWN):
-        halo(phi0, p0(image), rows0, own_rows[image - FIRST])
+    halos(phi0, rows0, own_slots)
     live_round(0)
     each(every, drift0)
     each(mids, gap0)
     live_round(1)
 
     arrive(0)
-    rows = {image: send_rows(phi0, p0(image), rows0) for image in (3, 8)}
+    slots = [p0(image) for image in (3, 8)]
+    send_rows(phi0, rows0, slots)
     each(ends, gap0)
     move = exchange(mine0, theirs0, 0, OWN)
-    for image in (3, 8):
-        halo(phi0, p0(image), rows0, rows[image])
+    halos(phi0, rows0, slots)
     move.wait_recv()
     speeds(mine0, theirs0, 0, OWN, speed0)
     each(every, theta0)
@@ -362,11 +363,11 @@
     live_round(2)
 
     arrive(1)
-    rows = {image: send_rows(phi0, p0(image), rows0) for image in (2, 9)}
+    slots = [p0(image) for image in (2, 9)]
+    send_rows(phi0, rows0, slots)
     each(outs, gap0)
     move = exchange(mine0, theirs0, OWN, 2)
-    for image in (2, 9):
-        halo(phi0, p0(image), rows0, rows[image])
+    halos(phi0, rows0, slots)
     move.wait_recv()
     speeds(mine0, theirs0, OWN, 2, speed0)
     each(outs, theta0)
@@ -388,19 +389,19 @@
     live_round(3)
 
     arrive(2)
-    rows = {image: send_rows(phi1, p1(image), rows1) for image in (2, 9)}
+    slots = [p1(image) for image in (2, 9)]
+    send_rows(phi1, rows1, slots)
     each(outs, gap1)
-    for image in (2, 9):
-        halo(phi1, p1(image), rows1, rows[image])
+    halos(phi1, rows1, slots)
     for image in (2, 9):
         drift(phi1, th1, p1(image), t1(image), slab)
 
     arrive(3)
-    rows = {image: send_rows(phi1, p1(image), rows1) for image in (3, 8)}
+    slots = [p1(image) for image in (3, 8)]
+    send_rows(phi1, rows1, slots)
     each(ends, gap1)
     move = exchange(mine1, theirs1, 2, 2)
-    for image in (3, 8):
-        halo(phi1, p1(image), rows1, rows[image])
+    halos(phi1, rows1, slots)
     each(outs, drift1)
     last_move = exchange(mine1, theirs1, 4, 2)
     move.wait_recv()
@@ -440,7 +441,7 @@
     live_round(4)
 
     def send_length(k):
-        return remote(message.at[0], gathered.at[img], len_send.at[k], len_recv.at[k], {"img": lax.rem(img + k, count)})
+        return remote(message.at[0], gathered.at[img], len_sem.at[0], len_sem.at[1], {"img": lax.rem(img + k, count)})
 
     def spread_out(i, carry):
         distance = count // 2 - 1 - i
@@ -458,21 +459,23 @@
     arrive(5)
     cross(lower_half, upper_half)
 
-    when(has_low, down + paces[:1], "wait_send")
-    when(has_high, up + paces[1:], "wait_send")
-    for copy in row_moves + swaps:
+    crossed = part(phi1, pl.ds(0, 5))
+    pl.when(has_low)(lambda: take(crossed, side_send.at[0]))
+    pl.when(has_high)(lambda: take(crossed, side_send.at[1]))
+    when(has_low, paces[:1], "wait_send")
+    when(has_high, paces[1:], "wait_send")
+    for n, group in enumerate(groups):
+        take(group, row_send.at[n])
+    for copy in swaps:
         copy.wait_send()
 
-    def heard(k, carry):
-        send_length(k).wait_send()
-        send_length(k).wait_recv()
-        return carry
-
-    hand_over = remote(gathered, lengths, sum_send.at[7], sum_recv.at[7], to_partner)
+    hand_over = remote(gathered, lengths, sum_send.at[6], sum_recv.at[6], to_partner)
 
     @pl.when(core == 1)
     def _():
-        lax.fori_loop(1, count, heard, 0)
+        others = gathered.at[pl.ds(0, count - 1)]
+        take(others, len_sem.at[0])
+        take(others, len_sem.at[1])
         hand_over.start()
         lengths[...] = gathered[...]
 
@@ -501,7 +504,7 @@
         weights.append(jnp.broadcast_to((target - arc) / seg, (SUB, half)))
 
     for t in range(TILES):
-        when(has_high, [down_new[0][t], down_new[1][t]], "wait_recv")
+        pl.when(has_high)(lambda t=t: take(phi2[t].at[pl.ds(0, 2)], new_recv.at[0, t]))
         when(has_low, [up_new[t]], "wait_recv")
         for i in range(OWN):
             pick = jnp.clip(bracket[i] - (OWN * img - 2), 0, 7)
@@ -510,8 +513,8 @@
                 base = phi2[t][pick, :, span]
                 out[i, t, :, span] = base + weights[i] * (phi2[t][pick + 1, :, span] - base)
 
-    when(has_low, down_new[0] + down_new[1], "wait_send")
-    when(has_high, up_new, "wait_send")
+    pl.when(has_low)(lambda: take(part(phi1, pl.ds(0, 2)), new_send.at[0]))
+    pl.when(has_high)(lambda: take(part(phi1, 0), new_send.at[1]))
     pl.when(core == 1)(hand_over.wait_send)
 
 
@@ -548,14 +551,14 @@
             pltpu.VMEM((count, 1, LANES), f32),
             pltpu.VMEM((count, 1, LANES), f32),
             dma((OWN,)),
-            dma((6,)), dma((6,)), dma((6,)), dma((6,)),
-            dma((24,)), dma((24,)),
-            dma((8,)), dma((8,)),
-            dma((3, TILES)), dma((3, TILES)),
+            dma((2,)), dma((6,)), dma((6,)),
+            dma((5,)), dma((5,)),
+            dma((7,)), dma((7,)),
+            dma((2,)), dma((2, TILES)),
             dma((2,)), dma((2,)),
-            dma((count,)), dma((count,)),
+            dma((2,)),
             pltpu.SMEM((images,), jnp.int32), dma,
-            pltpu.SemaphoreType.REGULAR((8,)),
+            pltpu.SemaphoreType.REGULAR((5,)),
         ],
         compiler_params=pltpu.CompilerParams(
             collective_id=0, has_side_effects=True, vmem_limit_bytes=40 * 1024 * 1024

time: 94.7 us -> 93.6 us (0.988)
  Pallas kernels: 93.3 us -> 92.1 us
    pallas_call x1, Pallas kernels: 93.3 us -> 92.1 us  [per_device(): pl.pallas_call(functools.partial(kernel, count), out_shape=jax.ShapeDtype...]
where the time goes in v5:
time: 93.6 us; the launch traced here: 93.5 us
  Pallas kernels  92.1 us (98%)
  local copies, waits for them, and re-layouts  1.32 us (1%)
    pallas_call x1, Pallas kernels, per_device(): pl.pallas_call(functools.partial(kernel, count), out_shape=jax.ShapeDtype...  92.1 us

profile of v5, /device:TPU:37, one launch (start us, length us, event | category | flops | bytes accessed | tf_op | source)
XLA Modules:
  0.0 93.5 jit_solution(12686779150819514253)
XLA Ops:
  0.0 92.1 %shard_map.28 = f32[4,4,8,4096]{3,2,1,0:T(8,128)S(1)} custom-call(f32[4,4,8,4096]{3,2,1,0:T(8,128)} %bitcast.3, s32[4]{0:T(128)} %given.1), custom_call_target="tpu_custom_call" | custom-call | tf_op jit(solution)/shard_map/pallas_call | solution.py:533
  92.1 1.3 %copy.4 = f32[4,32,4096]{2,1,0:T(8,128)} copy(f32[4,32,4096]{2,1,0:T(8,128)S(1)} %bitcast.2) | data formatting | bytes 4194304

commit v6 on v5

--- a/solution.py
+++ b/solution.py
@@ -32,7 +32,7 @@
 
 
 def kernel(count, path, given, out, phi0, phi1, phi2_0, phi2_1, phi2_2, phi2_3, th0, th1, rows0, rows1,
-           mine0, theirs0, mine1, theirs1, mine2, theirs2, speed0, speed1, message, gathered, lengths,
+           mine0, theirs0, mine1, theirs1, mine2, theirs2, speed0, speed1, message, gathered,
            local_sem, side_send, down_recv, up_recv, row_send, row_recv, sum_send, sum_recv,
            new_send, new_recv, pace_send, pace_recv, len_sem, bracket, given_sem, live):
     cols = path.shape[-1]
@@ -60,10 +60,7 @@
     loads = [
         pltpu.make_async_copy(path.at[i], phi0.at[p0(FIRST + i), pl.ds(0, TILES)], local_sem.at[i]) for i in range(OWN)
     ]
-    for i in (0, 3, 1, 2):
-        loads[i].start()
     given_load = pltpu.make_async_copy(given, bracket, given_sem)
-    given_load.start()
 
     barrier = pltpu.get_barrier_semaphore()
     def signal(sem, where):
@@ -72,6 +69,9 @@
     has_low, has_high = img > 0, img < count - 1
     pl.when(has_low)(lambda: signal(barrier, to_low))
     pl.when(has_high)(lambda: signal(barrier, to_high))
+    for i in (0, 3, 1, 2):
+        loads[i].start()
+    given_load.start()
     neighbours = has_low.astype(jnp.int32) + has_high.astype(jnp.int32)
     pl.semaphore_wait(barrier, neighbours + (1 - core))
     signal(barrier, to_partner)
@@ -414,6 +414,8 @@
     each(ends, next2)
     for image in (5, 6, 7):
         segment_sum(image, mine2.at[image - FIRST])
+    when(has_low & (core == 0), down_new[0], "start")
+    when(has_high & (core == 0), up_new, "start")
 
     when(has_high, [paces[0]], "wait_recv")
     when(has_low, [paces[1]], "wait_recv")
@@ -441,23 +443,38 @@
     live_round(4)
 
     def send_length(k):
-        return remote(message.at[0], gathered.at[img], len_sem.at[0], len_sem.at[1], {"img": lax.rem(img + k, count)})
+        for side in (0, 1):
+            remote(message.at[0], gathered.at[img], len_sem.at[side], len_sem.at[2],
+                   {"img": lax.rem(img + k, count), "space": side}).start()
 
     def spread_out(i, carry):
         distance = count // 2 - 1 - i
-        send_length(distance).start()
-        send_length(count - distance).start()
+        send_length(distance)
+        send_length(count - distance)
         return carry
 
     @pl.when(core == 1)
     def _():
-        send_length(count // 2).start()
+        send_length(count // 2)
         lax.fori_loop(0, count // 2 - 1, spread_out, 0)
 
-    go_down(*down_new[0], *down_new[1])
-    go_up(*up_new)
+    when(has_low & (core == 1), down_new[0] + down_new[1], "start")
+    when(has_high & (core == 1), up_new, "start")
     arrive(5)
     cross(lower_half, upper_half)
+
+    sent_down = part(phi1, pl.ds(0, 2))
+    turn = live.at[5]
+
+    @pl.when(core == 1)
+    def _():
+        pl.when(has_low)(lambda: take(sent_down, new_send.at[0]))
+        signal(turn, to_partner)
+
+    @pl.when(core == 0)
+    def _():
+        pl.semaphore_wait(turn, 1)
+        when(has_low, down_new[1], "start")
 
     crossed = part(phi1, pl.ds(0, 5))
     pl.when(has_low)(lambda: take(crossed, side_send.at[0]))
@@ -469,22 +486,19 @@
     for copy in swaps:
         copy.wait_send()
 
-    hand_over = remote(gathered, lengths, sum_send.at[6], sum_recv.at[6], to_partner)
+    others = gathered.at[pl.ds(0, count - 1)]
 
     @pl.when(core == 1)
     def _():
-        others = gathered.at[pl.ds(0, count - 1)]
         take(others, len_sem.at[0])
         take(others, len_sem.at[1])
-        hand_over.start()
-        lengths[...] = gathered[...]
-
-    pl.when(core == 0)(hand_over.wait_recv)
+
+    take(others, len_sem.at[2])
 
     owner = lax.broadcasted_iota(jnp.int32, (count, 1, LANES), 0)
     spot = lax.broadcasted_iota(jnp.int32, (count, 1, LANES), 2)
     index = OWN * owner + spot
-    squares = lengths[...]
+    squares = gathered[...]
     before = jnp.concatenate([squares[count - 1 :], squares[: count - 1]], axis=0)
     halves = jnp.where(spot == 0, squares, 0.0) + jnp.where(spot == OWN, before, 0.0)
     squares = jnp.where(spot == 0, jnp.sum(halves, axis=2, keepdims=True), squares)
@@ -513,9 +527,8 @@
                 base = phi2[t][pick, :, span]
                 out[i, t, :, span] = base + weights[i] * (phi2[t][pick + 1, :, span] - base)
 
-    pl.when(has_low)(lambda: take(part(phi1, pl.ds(0, 2)), new_send.at[0]))
+    pl.when(has_low & (core == 0))(lambda: take(sent_down, new_send.at[0]))
     pl.when(has_high)(lambda: take(part(phi1, 0), new_send.at[1]))
-    pl.when(core == 1)(hand_over.wait_send)
 
 
 def per_device(count, path, bracket):
@@ -549,16 +562,15 @@
             small(6), small(8),
             pltpu.VMEM((1, 1, LANES), f32),
             pltpu.VMEM((count, 1, LANES), f32),
-            pltpu.VMEM((count, 1, LANES), f32),
             dma((OWN,)),
             dma((2,)), dma((6,)), dma((6,)),
             dma((5,)), dma((5,)),
-            dma((7,)), dma((7,)),
+            dma((6,)), dma((6,)),
             dma((2,)), dma((2, TILES)),
             dma((2,)), dma((2,)),
-            dma((2,)),
+            dma((3,)),
             pltpu.SMEM((images,), jnp.int32), dma,
-            pltpu.SemaphoreType.REGULAR((5,)),
+            pltpu.SemaphoreType.REGULAR((6,)),
         ],
         compiler_params=pltpu.CompilerParams(
             collective_id=0, has_side_effects=True, vmem_limit_bytes=40 * 1024 * 1024

time: 93.6 us -> 93 us (level)
  Pallas kernels: 92.1 us -> 91 us
    pallas_call x1, Pallas kernels: 92.1 us -> 91 us  [per_device(): pl.pallas_call(functools.partial(kernel, count), out_shape=jax.ShapeDtype...]
where the time goes in v6:
time: 93 us; the launch traced here: 92.3 us
  Pallas kernels  91 us (98%)
  local copies, waits for them, and re-layouts  1.32 us (1%)
    pallas_call x1, Pallas kernels, per_device(): pl.pallas_call(functools.partial(kernel, count), out_shape=jax.ShapeDtype...  91 us

profile of v6, /device:TPU:37, one launch (start us, length us, event | category | flops | bytes accessed | tf_op | source)
XLA Modules:
  0.0 92.3 jit_solution(17602076244318725833)
XLA Ops:
  0.0 91.0 %shard_map.28 = f32[4,4,8,4096]{3,2,1,0:T(8,128)S(1)} custom-call(f32[4,4,8,4096]{3,2,1,0:T(8,128)} %bitcast.3, s32[4]{0:T(128)} %given.1), custom_call_target="tpu_custom_call" | custom-call | tf_op jit(solution)/shard_map/pallas_call | solution.py:546
  91.0 1.3 %copy.4 = f32[4,32,4096]{2,1,0:T(8,128)} copy(f32[4,32,4096]{2,1,0:T(8,128)S(1)} %bitcast.2) | data formatting | bytes 4194304

commit v7 on v6

--- a/solution.py
+++ b/solution.py
@@ -101,7 +101,8 @@
         shift(phi1, p1, 5, 1, 4, to_high, 0, 2), shift(phi1, p1, 5, 1, 5, to_high, 2, 2),
     ]
     down_new = [
-        [remote(phi2[t].at[p2(source)], phi2[t].at[p2(target)], new_send.at[0], new_recv.at[0, t], to_low)
+        [remote(phi2[t].at[p2(source)], phi2[t].at[p2(target)],
+                new_send.at[2 if (source, t) == (6, TILES - 1) else 0], new_recv.at[0, t], to_low)
          for t in range(TILES)]
         for source, target in ((5, 9), (6, 10))
     ]
@@ -463,7 +464,7 @@
     arrive(5)
     cross(lower_half, upper_half)
 
-    sent_down = part(phi1, pl.ds(0, 2))
+    sent_down = phi2[0].at[pl.ds(0, 2 * TILES - 1)]
     turn = live.at[5]
 
     @pl.when(core == 1)
@@ -528,6 +529,7 @@
                 out[i, t, :, span] = base + weights[i] * (phi2[t][pick + 1, :, span] - base)
 
     pl.when(has_low & (core == 0))(lambda: take(sent_down, new_send.at[0]))
+    when(has_low, down_new[1][TILES - 1 :], "wait_send")
     pl.when(has_high)(lambda: take(part(phi1, 0), new_send.at[1]))
 
 
@@ -566,7 +568,7 @@
             dma((2,)), dma((6,)), dma((6,)),
             dma((5,)), dma((5,)),
             dma((6,)), dma((6,)),
-            dma((2,)), dma((2, TILES)),
+            dma((3,)), dma((2, TILES)),
             dma((2,)), dma((2,)),
             dma((3,)),
             pltpu.SMEM((images,), jnp.int32), dma,

time: 93 us -> 92.4 us (level)
  no operation moved by 1% of the time
where the time goes in v7:
time: 92.4 us; the launch traced here: 92.3 us
  Pallas kernels  91 us (98%)
  local copies, waits for them, and re-layouts  1.32 us (1%)
    pallas_call x1, Pallas kernels, per_device(): pl.pallas_call(functools.partial(kernel, count), out_shape=jax.ShapeDtype...  91 us

profile of v7, /device:TPU:37, one launch (start us, length us, event | category | flops | bytes accessed | tf_op | source)
XLA Modules:
  0.0 92.3 jit_solution(3377221981889710883)
XLA Ops:
  0.0 91.0 %shard_map.28 = f32[4,4,8,4096]{3,2,1,0:T(8,128)S(1)} custom-call(f32[4,4,8,4096]{3,2,1,0:T(8,128)} %bitcast.3, s32[4]{0:T(128)} %given.1), custom_call_target="tpu_custom_call" | custom-call | tf_op jit(solution)/shard_map/pallas_call | solution.py:548
  91.0 1.3 %copy.4 = f32[4,32,4096]{2,1,0:T(8,128)} copy(f32[4,32,4096]{2,1,0:T(8,128)S(1)} %bitcast.2) | data formatting | bytes 4194304
